TPU v7x, 32 devices: a whole 2x2x4 slice. The times are simulated.
32 devices in a mesh: dp: 8 (over z, x), cls: 4 (over y, core).
Axes of the slice: x: 2, y: 2, z: 4, core: 2. Of those that a mesh axis runs over, the one named last changes fastest.
Arguments:
- embeddings: bfloat16 [24576, 768], P('dp'), may hold values from -6 to 6
- labels: int32 [24576], P('dp'), may hold values from 0 to 2751, as said below
- row_count: int32 [8], P('dp'), may hold values from 768 to 3072
Outputs:
- class_means: float32 [2752, 768], P(('dp', 'cls'))
- prototypes: float32 [2752, 768], P(('dp', 'cls'))
- similarity: float32 [24576], P('dp')
Inputs may be any that keep to these rules, and one draw needn't show every extreme that they name: Rows of index i of dp at or beyond row_count[i] are padding. `labels`: classes c and c' belong to the same block when c // 86 == c' // 86; block b belongs to index b mod 4 of cls. The rows of one index of dp name at most 16 distinct classes of any one block. Some block has exactly 16 of its classes named by the rows of every index of dp. The rows of some index of dp name exactly 16 classes of every block of some index of cls.
All inputs are finite; a program needn't handle non-finite values.
Results may differ from a plain program's by a relative error of at most 0.0017.
Values sent between devices are 32-bit elements; how exact they have to be, the bound alone decides.
No kernel may reach another device: no remote copies, remote signals or barrier semaphores. Data moves between devices by JAX's collectives and lax.ppermute only.
A program may use at most 64 MiB of HBM per device.

v0:
```python
import jax
import jax.numpy as jnp
from jax import lax
from jax.sharding import PartitionSpec as P

CLS_DEV = 86
SLOTS = 16


epsilon = 1e-06
sharpness = 4.0


def normalize(matrix):
    return matrix / jnp.sqrt(jnp.sum(matrix * matrix, axis=1, keepdims=True) + epsilon)


def slot_tables(counts, owner_count):
    present = (counts > 0).reshape(owner_count, CLS_DEV)
    rank = jnp.cumsum(present.astype(jnp.int32), axis=1) - 1
    slot_iota = lax.iota(jnp.int32, SLOTS)
    class_iota = lax.iota(jnp.int32, CLS_DEV)
    match = present[:, None, :] & (rank[:, None, :] == slot_iota[None, :, None])
    filled = jnp.any(match, axis=2)
    chosen = jnp.sum(jnp.where(match, class_iota[None, None, :], 0), axis=2)
    source = lax.iota(jnp.int32, owner_count)[:, None] * CLS_DEV + chosen
    slot_ids = jnp.where(filled, chosen.astype(jnp.float32), -1.0)
    return (source, filled, slot_ids)


def pack_rows(table, source, filled):
    picked = jnp.take(table, source.reshape(-1), axis=0).reshape(filled.shape + (table.shape[1],))
    return jnp.where(filled[:, :, None], picked, 0.0)


def spread_rows(received, received_ids):
    flat_ids = received_ids.reshape(-1)
    onehot = (flat_ids[:, None] == lax.iota(jnp.float32, CLS_DEV)[None, :]).astype(jnp.float32)
    flat_rows = received.reshape(flat_ids.shape[0], -1)
    return lax.dot_general(
        onehot,
        flat_rows,
        (((0,), (0,)), ((), ())),
        precision=lax.Precision.HIGHEST,
        preferred_element_type=jnp.float32,
    )


def gather_units(class_means):
    return lax.all_gather(normalize(class_means), "dp", axis=0, tiled=True)


def shards(embeddings, labels, row_count):
    row_total = embeddings.shape[0]
    feature_width = embeddings.shape[1]
    group_count = lax.axis_size("cls")
    owner_count = lax.axis_size("dp")
    table_width = CLS_DEV * owner_count
    tile_rows = min(512, row_total)
    position = lax.iota(jnp.int32, row_total)
    alive = position < row_count[0]
    class_group = labels // CLS_DEV
    owned = (class_group % group_count == lax.axis_index("cls")) & alive
    local_label = jnp.where(owned, class_group // group_count * CLS_DEV + labels % CLS_DEV, -1)
    turns = row_total // tile_rows
    columns = lax.iota(jnp.int32, table_width)
    nothing = jnp.zeros((), jnp.bfloat16)

    def accumulate(weights, with_counts):

        def advance(turn, state_pair):
            running, counts = state_pair
            first_row = turn * tile_rows
            row_piece = lax.dynamic_slice_in_dim(embeddings, first_row, tile_rows, 0)
            tile_labels = lax.dynamic_slice_in_dim(local_label, first_row, tile_rows, 0)
            tile_weights = lax.dynamic_slice_in_dim(weights, first_row, tile_rows, 0)
            onehot = jnp.where(
                tile_labels[:, None] == columns[None, :], tile_weights[:, None], nothing
            )
            running = running + lax.dot_general(
                onehot, row_piece, (((0,), (0,)), ((), ())), preferred_element_type=jnp.float32
            )
            if with_counts:
                counts = counts + jnp.sum(onehot.astype(jnp.float32), axis=0)
            return (running, counts)

        start_pair = (
            jnp.zeros((table_width, feature_width), jnp.float32),
            jnp.zeros((table_width,), jnp.float32),
        )
        return lax.fori_loop(0, turns, advance, start_pair)

    class_sums, counts = accumulate(jnp.ones((row_total,), jnp.bfloat16), True)
    source, filled, slot_ids = slot_tables(counts, owner_count)
    own_sums, own_counts = (
        lax.psum_scatter(class_sums, "dp", scatter_dimension=0, tiled=True),
        lax.psum_scatter(counts, "dp", scatter_dimension=0, tiled=True),
    )
    class_means = own_sums / jnp.maximum(own_counts, 1.0)[:, None]
    unit_table = gather_units(class_means)
    features = embeddings.astype(jnp.float32)
    lengths = jnp.sqrt(jnp.sum(features * features, axis=1) + epsilon)
    lookup = jnp.take(unit_table, jnp.maximum(local_label, 0), axis=0)
    own_product = jnp.where(owned, jnp.sum(features * lookup, axis=1), 0.0)
    full_product = lax.psum(own_product, "cls")
    similarity = jnp.where(alive, full_product / lengths, 0.0)
    weight = jnp.where(alive, jnp.exp(sharpness * (similarity - 1.0)), 0.0).astype(jnp.bfloat16)
    weighted, unused = accumulate(weight, False)
    weighted_slots = pack_rows(weighted, source, filled)
    got_weighted, got_labels = (
        lax.all_to_all(weighted_slots, "dp", split_axis=0, concat_axis=0, tiled=True),
        lax.all_to_all(slot_ids, "dp", split_axis=0, concat_axis=0, tiled=True),
    )
    own_weighted = spread_rows(got_weighted, got_labels)
    prototypes = normalize(own_weighted)
    return (class_means, prototypes, similarity)


def solution(mesh):
    in_specs = (P("dp", None), P("dp"), P("dp"))
    out_specs = (P(("dp", "cls"), None), P(("dp", "cls"), None), P("dp"))
    return jax.shard_map(shards, mesh=mesh, in_specs=in_specs, out_specs=out_specs, check_vma=False)
```

profile of v0, /device:TPU:0, one launch (start us, length us, event | category | flops | bytes accessed | tf_op | source)
XLA Modules:
  0.0 224.0 jit_solution(5737835677330729141)
XLA Ops:
  7.9 0.7 maximum_compare_fusion
  8.6 15.6 %while.30 = (s32[]{:T(128)}, f32[688,768]{1,0:T(8,128)S(1)}, f32[688]{0:T(1024)S(1)}, s32[3072]{0:T(1024)S(1)}, bf16[3072,768]{1,0:T(8,128)(2,1)}, /*index=5*/s32[]{:T(128)}, s32[]{:T(128)}, s32[]{:T(128)}, s32[]{:T(128)}) while((s32[]{:T(128)}, f32[688,768]{1,0:T(8,128)S(1)}, f32[688]{0:T(1024)S(1)}, s32[3072]{0:T(1024)S(1)}, ...), condition=%wide.region_2.3_spmd.clone, body=%wide.region_0.2_spmd.clone.sunk | while | flops 544236160 | bytes 5032862 | solution.py:91
  8.7 2.3 %select_add_fusion.6 = f32[688,768]{1,0:T(8,128)S(1)} fusion(f32[688,768]{1,0:T(8,128)S(1)} %get-tuple-element.372, pred[]{:T(512)S(6)} %compare.9, bf16[3072,768]{1,0:T(8,128)(2,1)} %get-tuple-element.384, s32[]{:T(128)S(6)} %select_n.190, s32[512]{0:T(512)S(1)} %dynamic_slice.50), kind=kOutput, calls=%fused_computation.4.clone.1 | convolution fusion | flops 542826496 | bytes 5015557 | tf_op jit(solution)/shard_map/while/body/eval_jaxpr/dot_general | solution.py:80
  11.0 0.2 convert_reduce_fusion.2
  11.3 2.3 %select_add_fusion.6 = f32[688,768]{1,0:T(8,128)S(1)} fusion(f32[688,768]{1,0:T(8,128)S(1)} %get-tuple-element.372, pred[]{:T(512)S(6)} %compare.9, bf16[3072,768]{1,0:T(8,128)(2,1)} %get-tuple-element.384, s32[]{:T(128)S(6)} %select_n.190, s32[512]{0:T(512)S(1)} %dynamic_slice.50), kind=kOutput, calls=%fused_computation.4.clone.1 | convolution fusion | flops 542826496 | bytes 5015557 | tf_op jit(solution)/shard_map/while/body/eval_jaxpr/dot_general | solution.py:80
  13.6 0.2 convert_reduce_fusion.2
  13.9 2.3 %select_add_fusion.6 = f32[688,768]{1,0:T(8,128)S(1)} fusion(f32[688,768]{1,0:T(8,128)S(1)} %get-tuple-element.372, pred[]{:T(512)S(6)} %compare.9, bf16[3072,768]{1,0:T(8,128)(2,1)} %get-tuple-element.384, s32[]{:T(128)S(6)} %select_n.190, s32[512]{0:T(512)S(1)} %dynamic_slice.50), kind=kOutput, calls=%fused_computation.4.clone.1 | convolution fusion | flops 542826496 | bytes 5015557 | tf_op jit(solution)/shard_map/while/body/eval_jaxpr/dot_general | solution.py:80
  16.2 0.2 convert_reduce_fusion.2
  16.5 2.3 %select_add_fusion.6 = f32[688,768]{1,0:T(8,128)S(1)} fusion(f32[688,768]{1,0:T(8,128)S(1)} %get-tuple-element.372, pred[]{:T(512)S(6)} %compare.9, bf16[3072,768]{1,0:T(8,128)(2,1)} %get-tuple-element.384, s32[]{:T(128)S(6)} %select_n.190, s32[512]{0:T(512)S(1)} %dynamic_slice.50), kind=kOutput, calls=%fused_computation.4.clone.1 | convolution fusion | flops 542826496 | bytes 5015557 | tf_op jit(solution)/shard_map/while/body/eval_jaxpr/dot_general | solution.py:80
  18.8 0.2 convert_reduce_fusion.2
  19.1 2.3 %select_add_fusion.6 = f32[688,768]{1,0:T(8,128)S(1)} fusion(f32[688,768]{1,0:T(8,128)S(1)} %get-tuple-element.372, pred[]{:T(512)S(6)} %compare.9, bf16[3072,768]{1,0:T(8,128)(2,1)} %get-tuple-element.384, s32[]{:T(128)S(6)} %select_n.190, s32[512]{0:T(512)S(1)} %dynamic_slice.50), kind=kOutput, calls=%fused_computation.4.clone.1 | convolution fusion | flops 542826496 | bytes 5015557 | tf_op jit(solution)/shard_map/while/body/eval_jaxpr/dot_general | solution.py:80
  21.4 0.2 convert_reduce_fusion.2
  21.8 2.3 %select_add_fusion.6 = f32[688,768]{1,0:T(8,128)S(1)} fusion(f32[688,768]{1,0:T(8,128)S(1)} %get-tuple-element.372, pred[]{:T(512)S(6)} %compare.9, bf16[3072,768]{1,0:T(8,128)(2,1)} %get-tuple-element.384, s32[]{:T(128)S(6)} %select_n.190, s32[512]{0:T(512)S(1)} %dynamic_slice.50), kind=kOutput, calls=%fused_computation.4.clone.1 | convolution fusion | flops 542826496 | bytes 5015557 | tf_op jit(solution)/shard_map/while/body/eval_jaxpr/dot_general | solution.py:80
  24.0 0.2 convert_reduce_fusion.2
  24.3 50.9 %fusion.4 = f32[88,768]{1,0:T(8,128)S(1)} fusion(f32[688,768]{1,0:T(8,128)S(1)} %get-tuple-element.222), kind=kCustom, calls=%all-reduce-scatter | all-reduce-scatter fusion | flops 540673 | bytes 2384384
  75.2 1.3 collective-permute-start
  76.5 21.5 %all-reduce.1 = f32[688]{0:T(1024)S(1)} all-reduce(f32[688]{0:T(1024)S(1)} %get-tuple-element.223), channel_id=3, replica_groups=mesh['dp'=8,'cls'=4] {'dp'}, use_global_device_ids=true, to_apply=%region_4.5.clone | all-reduce | flops 688 | bytes 5504
  98.1 0.6 fusion.39
  100.0 0.2 concatenate
  100.3 0.9 multiply_reduce_fusion.1
  101.3 0.8 divide_bitcast_fusion
  102.1 0.1 and.46
  102.2 0.2 reduce_window_sum.11
  102.5 0.2 fusion.25
  102.7 0.2 select_reduce_fusion
  102.9 0.6 convert_select_fusion
  103.5 3.3 %all-to-all-start = ((f32[8,1,16]{2,1,0:T(1,128)}), f32[8,1,16]{2,1,0:T(1,128)S(1)}, u32[]{:S(2)}, u32[]{:S(2)}) async-start(f32[8,1,16]{2,1,0:T(1,128)} %bitcast.2), calls=%async_computation | async-start | bytes 8192 | tf_op jit(solution)/shard_map/all_to_all | solution.py:112
  107.1 42.2 %all-gather.3.cloned.1.call-done = f32[8,86,768]{2,1,0:T(8,128)} async-done(((f32[1,86,768]{2,1,0:T(8,128)}), f32[8,86,768]{2,1,0:T(8,128)}) %all-gather.3.cloned.1.call-update) | async-done | bytes 2113552 | tf_op jit(solution)/shard_map/all_gather | solution.py:50
  149.3 1.7 reshape.135
  151.0 13.8 %gather_fusion = f32[3072,768]{1,0:T(8,128)} fusion(f32[688,768]{1,0:T(8,128)S(1)} %reshape.135, s32[3072]{0:T(1024)S(1)} %maximum_clamp_fusion), kind=kCustom, calls=%fused_computation | custom fusion | bytes 18886656 | tf_op jit(solution)/shard_map/jit(_take)/gather | solution.py:103
  164.8 6.8 %fusion.23 = (f32[3072]{0:T(1024)S(1)}, f32[3072]{0:T(1024)S(1)}) fusion(bf16[3072,768]{1,0:T(8,128)(2,1)} %get-tuple-element.417, f32[3072,768]{1,0:T(8,128)} %gather_fusion, pred[3072]{0:T(1024)(128)(4,1)S(1)} %get-tuple-element.291), kind=kLoop, calls=%fused_computation.28 | loop fusion | flops 14149632 | bytes 14183424 | tf_op jit(solution)/shard_map/reduce_sum | solution.py:102
  171.6 10.1 %psum.7 = f32[3072]{0:T(1024)S(1)} all-reduce(f32[3072]{0:T(1024)S(1)} %broadcast_select_fusion), channel_id=1, replica_groups=mesh['dp'=8,'cls'=4] {'cls'}, use_global_device_ids=true, to_apply=%region_10.11 | all-reduce | flops 3072 | bytes 24576 | tf_op jit(solution)/shard_map/psum | solution.py:105
  181.7 0.6 select_convert_fusion
  182.3 16.9 %while.31 = (s32[]{:T(128)}, f32[688,768]{1,0:T(8,128)S(1)}, s32[3072]{0:T(1024)S(1)}, bf16[3072]{0:T(1024)(128)(2,1)S(1)}, bf16[3072,768]{1,0:T(8,128)(2,1)}, /*index=5*/s32[]{:T(128)}, s32[]{:T(128)}, s32[]{:T(128)}, s32[]{:T(128)}) while((s32[]{:T(128)}, f32[688,768]{1,0:T(8,128)S(1)}, s32[3072]{0:T(1024)S(1)}, ...), condition=%wide.region_13.14_spmd.clone, body=%wide.region_12.13_spmd.clone.sunk | while | flops 542826496 | bytes 5022881 | solution.py:91
  182.5 2.6 %select_add_fusion.8 = f32[688,768]{1,0:T(8,128)S(1)} fusion(f32[688,768]{1,0:T(8,128)S(1)} %get-tuple-element.399, pred[]{:T(512)S(6)} %compare.10, bf16[3072,768]{1,0:T(8,128)(2,1)} %get-tuple-element.411, s32[]{:T(128)S(6)} %select_n.192, s32[512]{0:T(512)S(1)} %dynamic_slice.52, bf16[512]{0:T(512)(128)(2,1)S(1)} %dynamic_slice.53), kind=kOutput, calls=%fused_computation.16.clone.1 | convolution fusion | flops 542826496 | bytes 5016581 | tf_op jit(solution)/shard_map/while/body/eval_jaxpr/dot_general | solution.py:80
  185.3 2.6 %select_add_fusion.8 = f32[688,768]{1,0:T(8,128)S(1)} fusion(f32[688,768]{1,0:T(8,128)S(1)} %get-tuple-element.399, pred[]{:T(512)S(6)} %compare.10, bf16[3072,768]{1,0:T(8,128)(2,1)} %get-tuple-element.411, s32[]{:T(128)S(6)} %select_n.192, s32[512]{0:T(512)S(1)} %dynamic_slice.52, bf16[512]{0:T(512)(128)(2,1)S(1)} %dynamic_slice.53), kind=kOutput, calls=%fused_computation.16.clone.1 | convolution fusion | flops 542826496 | bytes 5016581 | tf_op jit(solution)/shard_map/while/body/eval_jaxpr/dot_general | solution.py:80
  188.1 2.6 %select_add_fusion.8 = f32[688,768]{1,0:T(8,128)S(1)} fusion(f32[688,768]{1,0:T(8,128)S(1)} %get-tuple-element.399, pred[]{:T(512)S(6)} %compare.10, bf16[3072,768]{1,0:T(8,128)(2,1)} %get-tuple-element.411, s32[]{:T(128)S(6)} %select_n.192, s32[512]{0:T(512)S(1)} %dynamic_slice.52, bf16[512]{0:T(512)(128)(2,1)S(1)} %dynamic_slice.53), kind=kOutput, calls=%fused_computation.16.clone.1 | convolution fusion | flops 542826496 | bytes 5016581 | tf_op jit(solution)/shard_map/while/body/eval_jaxpr/dot_general | solution.py:80
  190.9 2.6 %select_add_fusion.8 = f32[688,768]{1,0:T(8,128)S(1)} fusion(f32[688,768]{1,0:T(8,128)S(1)} %get-tuple-element.399, pred[]{:T(512)S(6)} %compare.10, bf16[3072,768]{1,0:T(8,128)(2,1)} %get-tuple-element.411, s32[]{:T(128)S(6)} %select_n.192, s32[512]{0:T(512)S(1)} %dynamic_slice.52, bf16[512]{0:T(512)(128)(2,1)S(1)} %dynamic_slice.53), kind=kOutput, calls=%fused_computation.16.clone.1 | convolution fusion | flops 542826496 | bytes 5016581 | tf_op jit(solution)/shard_map/while/body/eval_jaxpr/dot_general | solution.py:80
  193.7 2.6 %select_add_fusion.8 = f32[688,768]{1,0:T(8,128)S(1)} fusion(f32[688,768]{1,0:T(8,128)S(1)} %get-tuple-element.399, pred[]{:T(512)S(6)} %compare.10, bf16[3072,768]{1,0:T(8,128)(2,1)} %get-tuple-element.411, s32[]{:T(128)S(6)} %select_n.192, s32[512]{0:T(512)S(1)} %dynamic_slice.52, bf16[512]{0:T(512)(128)(2,1)S(1)} %dynamic_slice.53), kind=kOutput, calls=%fused_computation.16.clone.1 | convolution fusion | flops 542826496 | bytes 5016581 | tf_op jit(solution)/shard_map/while/body/eval_jaxpr/dot_general | solution.py:80
  196.6 2.6 %select_add_fusion.8 = f32[688,768]{1,0:T(8,128)S(1)} fusion(f32[688,768]{1,0:T(8,128)S(1)} %get-tuple-element.399, pred[]{:T(512)S(6)} %compare.10, bf16[3072,768]{1,0:T(8,128)(2,1)} %get-tuple-element.411, s32[]{:T(128)S(6)} %select_n.192, s32[512]{0:T(512)S(1)} %dynamic_slice.52, bf16[512]{0:T(512)(128)(2,1)S(1)} %dynamic_slice.53), kind=kOutput, calls=%fused_computation.16.clone.1 | convolution fusion | flops 542826496 | bytes 5016581 | tf_op jit(solution)/shard_map/while/body/eval_jaxpr/dot_general | solution.py:80
  199.2 0.8 gather_fusion.1
  200.0 0.9 select_select_fusion
  200.9 3.5 %all-to-all-start.1 = ((f32[8,16,768]{2,1,0:T(8,128)}), f32[8,16,768]{2,1,0:T(8,128)S(1)}, u32[]{:S(2)}, u32[]{:S(2)}) async-start(f32[8,16,768]{2,1,0:T(8,128)} %select_select_fusion), calls=%async_computation.1 | async-start | bytes 786432 | tf_op jit(solution)/shard_map/all_to_all | solution.py:111
  204.3 0.5 broadcast.158
  204.9 0.7 reduce.3
  205.6 10.2 %all-to-all-done.1 = f32[8,16,768]{2,1,0:T(8,128)S(1)} async-done(((f32[8,16,768]{2,1,0:T(8,128)}), f32[8,16,768]{2,1,0:T(8,128)S(1)}, u32[]{:S(2)}, u32[]{:S(2)}) %all-to-all-start.1) | async-done | bytes 393248 | tf_op jit(solution)/shard_map/all_to_all | solution.py:111
  215.8 0.5 multiply_reduce_fusion
  216.3 0.8 broadcast_divide_fusion
  (50 shorter events, 2.0 us)
Async XLA Ops:
  7.2 142.1 %all-gather.3.cloned.1.call-start = ((), (), s32[]{:S(2)}) async-start(), calls=%async_computation.2 | async-start | bytes 2433024 | tf_op jit(solution)/shard_map/all_gather | solution.py:50
  24.3 73.8 %copy-start.1 = (u32[32]{0:T(128)S(1)}, u32[32]{0:T(128)}, u32[]{:S(2)}) copy-start(u32[32]{0:T(128)} %constant.183) | copy-start | bytes 388
  75.2 24.8 %collective-permute-start = (f32[14,768]{1,0:T(8,128)S(1)}, f32[14,768]{1,0:T(8,128)S(1)}, u32[]{:S(2)}, u32[]{:S(2)}) collective-permute-start(f32[14,768]{1,0:T(8,128)S(1)} %slice.4), channel_id=1, source_target_pairs={{0,4},{4,8},{8,12},{12,16},{16,20},{20,24},{24,28},{1,5},{5,9},{9,... | collective-permute-start | bytes 129032
  103.5 97.4 %all-to-all-start = ((f32[8,1,16]{2,1,0:T(1,128)}), f32[8,1,16]{2,1,0:T(1,128)S(1)}, u32[]{:S(2)}, u32[]{:S(2)}) async-start(f32[8,1,16]{2,1,0:T(1,128)} %bitcast.2), calls=%async_computation | async-start | bytes 8192 | tf_op jit(solution)/shard_map/all_to_all | solution.py:112
  164.8 17.6 %copy-start = (f32[688,768]{1,0:T(8,128)S(1)}, f32[688,768]{1,0:T(8,128)}, u32[]{:S(2)}) copy-start(f32[688,768]{1,0:T(8,128)} %custom-call.2) | copy-start | bytes 6340612
  200.9 14.9 %all-to-all-start.1 = ((f32[8,16,768]{2,1,0:T(8,128)}), f32[8,16,768]{2,1,0:T(8,128)S(1)}, u32[]{:S(2)}, u32[]{:S(2)}) async-start(f32[8,16,768]{2,1,0:T(8,128)} %select_select_fusion), calls=%async_computation.1 | async-start | bytes 786432 | tf_op jit(solution)/shard_map/all_to_all | solution.py:111
Sparse Core Ops, SparseCore 0:
  102.2 46.9 all-gather.2
where the time goes:
time: 225 us; the launch traced here: 224 us
  blocking collectives  82.6 us (37%)
  waiting for transfers between devices  52.5 us (23%)
  matrix products  29.9 us (13%)
  local copies, waits for them, and re-layouts  19.3 us (9%)
  between operations  16.2 us (7%)
  other arithmetic  15.2 us (7%)
  starting transfers between devices  8.1 us (4%)
    unnamed x2, blocking collectives  72.4 us
    all_gather x1, waiting for transfers between devices, gather_units(): return lax.all_gather(normalize(class_means), 'dp', axis=0, tiled=True)  42.2 us
    dot_general x12, matrix products, advance(): lax.dot_general(onehot, row_piece, (((0,), (0,)), ((), ())), preferred_el...  29.4 us
    gather x1, local copies, waits for them, and re-layouts, shards(): lookup = jnp.take(unit_table, jnp.maximum(local_label, 0), axis=0)  13.8 us
    all_to_all x1, waiting for transfers between devices, shards(): lax.all_to_all(weighted_slots, 'dp', split_axis=0, concat_axis=0, tiled=T...  10.2 us
    psum x1, blocking collectives, shards(): full_product = lax.psum(own_product, 'cls')  10.1 us
    reduce_sum x1, other arithmetic, shards(): lengths = jnp.sqrt(jnp.sum(features * features, axis=1) + epsilon)  6.8 us
  transfers between devices with their start and end apart: 4, of which 2 were waited for; matrix products, arithmetic and copies ran while one was open for 20% of the time, Pallas kernels for 0%

commit v1 on v0

v1 whole, which is shorter than its diff:
```python
import functools

import jax
import jax.numpy as jnp
from jax import lax
from jax.experimental import pallas as pl
from jax.experimental.pallas import tpu as pltpu
from jax.sharding import PartitionSpec as P

CLS_DEV = 86
SLOTS = 16
LANES = 128
CLS_PAD = 96

epsilon = 1e-06
sharpness = 4.0

VMEM = pl.BlockSpec(memory_space=pltpu.VMEM)
SMEM = pl.BlockSpec(memory_space=pltpu.SMEM)
VMEM_LIMIT = 24 * 1024 * 1024


def dot(a, b, dims):
    return lax.dot_general(a, b, (dims, ((), ())), preferred_element_type=jnp.float32)


def split2(x):
    hi = x.astype(jnp.bfloat16)
    lo = (x - hi.astype(jnp.float32)).astype(jnp.bfloat16)
    return hi, lo


def split3(x):
    hi = x.astype(jnp.bfloat16)
    rest = x - hi.astype(jnp.float32)
    mid, lo = split2(rest)
    return hi, mid, lo


def flags(mask, dtype=jnp.bfloat16):
    return jnp.where(mask, 1.0, 0.0).astype(dtype)


def iota(shape, axis):
    return lax.broadcasted_iota(jnp.int32, shape, axis).astype(jnp.float32)


def put_slots(ref, rows):
    pieces = rows.shape[1] // LANES
    for owner in range(rows.shape[0] // SLOTS):
        for piece in range(pieces):
            ref[owner, piece * SLOTS:(piece + 1) * SLOTS, :] = rows[
                owner * SLOTS:(owner + 1) * SLOTS, piece * LANES:(piece + 1) * LANES
            ]


def get_slots(ref, pieces):
    rows = []
    for owner in range(ref.shape[0]):
        rows.append(
            jnp.concatenate(
                [ref[owner, piece * SLOTS:(piece + 1) * SLOTS, :] for piece in range(pieces)], axis=1
            )
        )
    return jnp.concatenate(rows, axis=0)


def sums_kernel(group_count, place_ref, label_ref, rows_ref, out_ref, slot_ref):
    owner_count = out_ref.shape[0]
    slot_total = owner_count * SLOTS
    row_total, width = rows_ref.shape
    pieces = width // LANES
    my_group, my_owner, live = place_ref[0], place_ref[1], place_ref[2]
    label = label_ref[...].astype(jnp.float32)
    block = jnp.floor((label + 0.5) * (1.0 / CLS_DEV))
    inner = label - block * CLS_DEV
    owner = jnp.floor((block + 0.5) * (1.0 / group_count))
    group = block - owner * group_count
    position = lax.broadcasted_iota(jnp.int32, (1, row_total), 1)
    owned = (group == my_group.astype(jnp.float32)) & (position < live)
    owner = jnp.where(owned, owner, -1.0)
    owner_pad = max(owner_count, 16)
    by_owner = iota((owner_pad, row_total), 0) == owner
    by_class = flags(iota((LANES, row_total), 0) == inner)
    counts = dot(flags(by_owner), by_class, ((1,), (1,)))
    present = counts > 0
    upto = flags(iota((LANES, LANES), 0) <= iota((LANES, LANES), 1))
    rank = dot(flags(present), upto, ((1,), (0,))) - 1.0
    slot = jnp.where(present, rank, -1.0)
    row_slots = dot(slot.astype(jnp.bfloat16), by_class, ((1,), (0,)))
    row_slot = jnp.sum(jnp.where(by_owner, row_slots, 0.0), axis=0, keepdims=True)
    where_to = jnp.where(owned, owner * SLOTS + row_slot, -1.0)
    slot_ref[...] = where_to
    onehot = flags(iota((slot_total, row_total), 0) == where_to)
    put_slots(out_ref, dot(onehot, rows_ref[...], ((1,), (0,))))
    class_at = iota((owner_pad, LANES), 1)
    lane = lax.broadcasted_iota(jnp.int32, (owner_pad, slot_total), 1) - my_owner * SLOTS
    ids = jnp.zeros((owner_pad, slot_total), jnp.float32)
    tally = jnp.zeros((owner_pad, slot_total), jnp.float32)
    for s in range(SLOTS):
        hit = slot == s
        chosen = jnp.sum(jnp.where(hit, class_at + 1.0, 0.0), axis=1, keepdims=True) - 1.0
        number = jnp.sum(jnp.where(hit, counts, 0.0), axis=1, keepdims=True)
        ids = jnp.where(lane == s, chosen, ids)
        tally = jnp.where(lane == s, number, tally)
    sub = lax.broadcasted_iota(jnp.int32, (8, LANES), 0)
    for o in range(owner_count):
        for t in range(slot_total // LANES):
            lanes = slice(t * LANES, (t + 1) * LANES)
            tile = jnp.where(sub == 0, ids[o:o + 1, lanes], jnp.where(sub == 1, tally[o:o + 1, lanes], 0.0))
            base = pieces * SLOTS + 8 * t
            out_ref[o, base:base + 8, :] = tile


def means_kernel(got_ref, means_ref, back_ref, ids_ref):
    owner_count = got_ref.shape[0]
    slot_total = owner_count * SLOTS
    width = means_ref.shape[1]
    pieces = width // LANES
    metas = []
    for t in range(slot_total // LANES):
        base = pieces * SLOTS + 8 * t
        meta = got_ref[0, base:base + 8, :]
        for o in range(1, owner_count):
            meta = meta + got_ref[o, base:base + 8, :]
        metas.append(meta)
    meta = jnp.concatenate(metas, axis=1)
    ids = meta[0:1, :]
    ids_ref[...] = ids
    match = iota((CLS_PAD, slot_total), 0) == ids
    counts = jnp.sum(jnp.where(match, meta[1:2, :], 0.0), axis=1, keepdims=True)
    onehot = flags(match)
    sums = sum(dot(onehot, part, ((1,), (0,))) for part in split3(get_slots(got_ref, pieces)))
    means = sums / jnp.maximum(counts, 1.0)
    means_ref[...] = means[:means_ref.shape[0]]
    unit = means / jnp.sqrt(jnp.sum(means * means, axis=1, keepdims=True) + epsilon)
    put_slots(back_ref, sum(dot(onehot, part, ((0,), (0,))) for part in split2(unit)))


def lengths_kernel(rows_ref, out_ref):
    row_total, width = rows_ref.shape
    tile = min(512, row_total)
    ones = jnp.ones((16, width), jnp.bfloat16)
    for t in range(row_total // tile):
        features = rows_ref[t * tile:(t + 1) * tile, :].astype(jnp.float32)
        hi, lo = split2(features * features)
        total = dot(ones, hi, ((1,), (1,))) + dot(ones, lo, ((1,), (1,)))
        out_ref[:, t * tile:(t + 1) * tile] = jnp.sqrt(total[0:1] + epsilon)


def weigh_kernel(unit_ref, rows_ref, slot_ref, length_ref, out_ref, sim_ref, acc_ref):
    row_total, width = rows_ref.shape
    slot_total = out_ref.shape[0] * SLOTS
    units = jnp.concatenate(split2(get_slots(unit_ref, width // LANES)), axis=0)
    tile = min(512, row_total)
    for t in range(row_total // tile):
        part = slice(t * tile, (t + 1) * tile)
        rows = rows_ref[part, :]
        products = dot(units, rows, ((1,), (1,)))
        where_to = slot_ref[:, part]
        hit = iota((slot_total, tile), 0) == where_to
        product = jnp.sum(
            jnp.where(hit, products[:slot_total] + products[slot_total:], 0.0), axis=0, keepdims=True
        )
        owned = where_to >= 0
        similarity = jnp.where(owned, product / length_ref[:, part], 0.0)
        sim_ref[:, part] = similarity
        weight = jnp.exp(sharpness * (similarity - 1.0))
        weights = jnp.where(hit, weight, 0.0).astype(jnp.bfloat16)
        weighted = dot(weights, rows, ((1,), (0,)))
        if t == 0:
            acc_ref[...] = weighted
        else:
            acc_ref[...] += weighted
    put_slots(out_ref, acc_ref[...])


def prototypes_kernel(got_ref, ids_ref, out_ref):
    slot_total = got_ref.shape[0] * SLOTS
    onehot = flags(iota((CLS_PAD, slot_total), 0) == ids_ref[...])
    rows = get_slots(got_ref, out_ref.shape[1] // LANES)
    weighted = sum(dot(onehot, part, ((1,), (0,))) for part in split3(rows))
    unit = weighted / jnp.sqrt(jnp.sum(weighted * weighted, axis=1, keepdims=True) + epsilon)
    out_ref[...] = unit[:out_ref.shape[0]]


def call(kernel, ins, outs, name, scratch=(), cost=None):
    return pl.pallas_call(
        kernel,
        in_specs=ins,
        out_specs=[VMEM] * len(outs),
        out_shape=[jax.ShapeDtypeStruct(shape, jnp.float32) for shape in outs],
        scratch_shapes=list(scratch),
        compiler_params=pltpu.CompilerParams(vmem_limit_bytes=VMEM_LIMIT),
        cost_estimate=cost,
        name=name,
    )


def exchange(payload):
    return lax.all_to_all(payload, "dp", split_axis=0, concat_axis=0, tiled=True)


def shards(embeddings, labels, row_count):
    row_total, width = embeddings.shape
    group_count = lax.axis_size("cls")
    owner_count = lax.axis_size("dp")
    slot_total = owner_count * SLOTS
    pieces = width // LANES
    slot_rows = pieces * SLOTS
    meta_rows = 8 * (slot_total // LANES)
    place = jnp.stack([lax.axis_index("cls"), lax.axis_index("dp"), row_count[0]]).astype(jnp.int32)
    payload, where_to = call(
        functools.partial(sums_kernel, group_count),
        [SMEM, VMEM, VMEM],
        [(owner_count, slot_rows + meta_rows, LANES), (1, row_total)],
        "sums",
    )(place, labels.reshape(1, row_total), embeddings)
    got = exchange(payload)
    cost = pl.CostEstimate(flops=8 * row_total * width * 128, bytes_accessed=2 * row_total * width, transcendentals=row_total)
    (lengths,) = call(lengths_kernel, [VMEM], [(1, row_total)], "lengths", cost=cost)(embeddings)
    class_means, back, ids = call(
        means_kernel,
        [VMEM],
        [(CLS_DEV, width), (owner_count, slot_rows, LANES), (1, slot_total)],
        "means",
    )(got)
    units = exchange(back)
    weighted, own_similarity = call(
        weigh_kernel,
        [VMEM] * 4,
        [(owner_count, slot_rows, LANES), (1, row_total)],
        "weigh",
        scratch=[pltpu.VMEM((slot_total, width), jnp.float32)],
    )(units, embeddings, where_to, lengths)
    got_weighted = exchange(weighted)
    own = own_similarity.reshape(row_total)
    similarity = own
    for step in range(1, group_count):
        ring = [(source, (source + step) % group_count) for source in range(group_count)]
        similarity = similarity + lax.ppermute(own, "cls", ring)
    (prototypes,) = call(prototypes_kernel, [VMEM] * 2, [(CLS_DEV, width)], "prototypes")(got_weighted, ids)
    return (class_means, prototypes, similarity)


def solution(mesh):
    in_specs = (P("dp", None), P("dp"), P("dp"))
    out_specs = (P(("dp", "cls"), None), P(("dp", "cls"), None), P("dp"))
    return jax.shard_map(shards, mesh=mesh, in_specs=in_specs, out_specs=out_specs, check_vma=False)
```

time: 225 us -> 66.1 us (0.29)
  blocking collectives: 82.6 us -> 19.7 us
  waiting for transfers between devices: 52.5 us -> 14.4 us
  matrix products: 29.9 us -> 0 us
  between operations: 16.2 us -> 1.33 us
  other arithmetic: 15.2 us -> 0.68 us
  Pallas kernels: 0 us -> 11.7 us
  local copies, waits for them, and re-layouts: 19.3 us -> 7.71 us
    unnamed x2 -> x0, blocking collectives: 72.4 us -> none
    all_gather x1 -> x0, waiting for transfers between devices: 42.2 us -> none  [gather_units(): return lax.all_gather(normalize(class_means), 'dp', axis=0, tiled=True)]
    dot_general x13 -> x0, matrix products: 29.9 us -> none  [the longest x12 29.4 us: advance(): lax.dot_general(onehot, row_piece, (((0,), (0,)), ((), ())), preferred_el...]
    all_to_all x0 -> x1, blocking collectives: none -> 19.7 us  [exchange(): lax.all_to_all(payload, 'dp', split_axis=0, concat_axis=0, tiled=True)]
    gather x2 -> x0, local copies, waits for them, and re-layouts: 14.6 us -> none  [the longest x1 13.8 us: shards(): lookup = jnp.take(unit_table, jnp.maximum(local_label, 0), axis=0)]
    pallas_call x0 -> x5, Pallas kernels: none -> 11.7 us  [the longest x1 4.27 us: shards(): call(weigh_kernel, [VMEM] * 4, [(owner_count, slot_rows, LANES), (1, row_...]
    psum x1 -> x0, blocking collectives: 10.1 us -> none  [shards(): full_product = lax.psum(own_product, 'cls')]
    reduce_sum x9 -> x0, other arithmetic: 9.27 us -> none  [the longest x1 6.8 us: shards(): lengths = jnp.sqrt(jnp.sum(features * features, axis=1) + epsilon)]
  transfers between devices with their start and end apart: 4 -> 5, of which waited for: 2 -> 5; matrix products, arithmetic and copies ran while one was open for 20% -> 1% of each run, Pallas kernels for 0% -> 4%
where the time goes in v1:
time: 66.1 us; the launch traced here: 65.6 us
  blocking collectives  19.7 us (30%)
  waiting for transfers between devices  14.4 us (22%)
  Pallas kernels  11.7 us (18%)
  starting transfers between devices  10.1 us (15%)
  local copies, waits for them, and re-layouts  7.71 us (12%)
  between operations  1.33 us (2%)
  other arithmetic  0.68 us (1%)
    all_to_all x1, blocking collectives, exchange(): lax.all_to_all(payload, 'dp', split_axis=0, concat_axis=0, tiled=True)  19.7 us
    all_to_all x2, waiting for transfers between devices, exchange(): lax.all_to_all(payload, 'dp', split_axis=0, concat_axis=0, tiled=True)  13 us
    unnamed x8, local copies, waits for them, and re-layouts  7.71 us
    all_to_all x2, starting transfers between devices, exchange(): lax.all_to_all(payload, 'dp', split_axis=0, concat_axis=0, tiled=True)  7.1 us
    pallas_call x1, Pallas kernels, shards(): call(weigh_kernel, [VMEM] * 4, [(owner_count, slot_rows, LANES), (1, row_...  4.27 us
    ppermute x3, starting transfers between devices, shards(): similarity = similarity + lax.ppermute(own, 'cls', ring)  2.98 us
    pallas_call x1, Pallas kernels, shards(): call(lengths_kernel, [VMEM], [(1, row_total)], 'lengths', cost=cost)  2.65 us
    pallas_call x1, Pallas kernels, shards(): call(functools.partial(sums_kernel, group_count), [SMEM, VMEM, VMEM], [(o...  2.24 us
  transfers between devices with their start and end apart: 5, of which 5 were waited for; matrix products, arithmetic and copies ran while one was open for 1% of the time, Pallas kernels for 4%

profile of v1, /device:TPU:0, one launch (start us, length us, event | category | flops | bytes accessed | tf_op | source)
XLA Modules:
  0.0 65.6 jit_solution(1608189576620043665)
XLA Ops:
  1.3 0.1 pad_add_fusion.place_ref
  1.4 0.0 copy-start
  1.4 2.3 %copy-done = bf16[3072,768]{1,0:T(8,128)(2,1)S(1)} copy-done((bf16[3072,768]{1,0:T(8,128)(2,1)S(1)}, bf16[3072,768]{1,0:T(8,128)(2,1)}, u32[]{:S(2)}) %copy-start) | copy-done | bytes 4718616
  3.7 0.0 copy-start.3
  3.7 0.7 %copy-done.3 = s32[3072]{0:T(1024)S(1)} copy-done((s32[3072]{0:T(1024)S(1)}, s32[3072]{0:T(1024)}, u32[]{:S(2)}) %copy-start.3) | copy-done | bytes 12312
  4.4 2.2 %sums.1 = (f32[8,104,128]{2,1,0:T(8,128)S(1)}, f32[1,3072]{1,0:T(1,128)S(1)}) custom-call(s32[3]{0:T(128)S(1)} %pad_add_fusion.place_ref, s32[1,3072]{1,0:T(1,128)S(1)} %bitcast.8, bf16[3072,768]{1,0:T(8,128)(2,1)S(1)} %copy-done), custom_call_target="tpu_custom_call" | custom-call | tf_op jit(solution)/shard_map/sums/pallas_call | solution.py:213
  6.6 19.7 %all_to_all.15.got_ref = f32[8,104,128]{2,1,0:T(8,128)S(1)} all-to-all(f32[8,104,128]{2,1,0:T(8,128)S(1)} %get-tuple-element.10), channel_id=1, replica_groups=mesh['dp'=8,'cls'=4] {'dp'}, dimensions={0} | all-to-all | bytes 851968 | tf_op jit(solution)/shard_map/all_to_all | solution.py:201
  26.3 1.4 %means.1 = (f32[86,768]{1,0:T(8,128)}, f32[8,96,128]{2,1,0:T(8,128)}, f32[1,128]{1,0:T(1,128)S(1)}) custom-call(f32[8,104,128]{2,1,0:T(8,128)S(1)} %all_to_all.15.got_ref), custom_call_target="tpu_custom_call" | custom-call | tf_op jit(solution)/shard_map/means/pallas_call | solution.py:222
  27.8 3.5 %all-to-all-start.1 = ((f32[8,96,128]{2,1,0:T(8,128)}), f32[8,96,128]{2,1,0:T(8,128)S(1)}, u32[]{:S(2)}, u32[]{:S(2)}) async-start(f32[8,96,128]{2,1,0:T(8,128)} %get-tuple-element.12), calls=%async_computation.1 | async-start | bytes 786432 | tf_op jit(solution)/shard_map/all_to_all | solution.py:201
  31.2 0.0 copy-start.1
  31.3 2.3 %copy-done.1 = bf16[3072,768]{1,0:T(8,128)(2,1)S(1)} copy-done((bf16[3072,768]{1,0:T(8,128)(2,1)S(1)}, bf16[3072,768]{1,0:T(8,128)(2,1)}, u32[]{:S(2)}) %copy-start.1) | copy-done | bytes 4718616
  33.6 2.7 %lengths.1.length_ref = f32[1,3072]{1,0:T(1,128)S(1)} custom-call(bf16[3072,768]{1,0:T(8,128)(2,1)S(1)} %copy-done.1), custom_call_target="tpu_custom_call" | custom-call | flops 2415919104 | bytes 4718592 | tf_op jit(solution)/shard_map/lengths/pallas_call | solution.py:221
  36.2 6.4 %all-to-all-done.1.unit_ref = f32[8,96,128]{2,1,0:T(8,128)S(1)} async-done(((f32[8,96,128]{2,1,0:T(8,128)}), f32[8,96,128]{2,1,0:T(8,128)S(1)}, u32[]{:S(2)}, u32[]{:S(2)}) %all-to-all-start.1) | async-done | bytes 393248 | tf_op jit(solution)/shard_map/all_to_all | solution.py:201
  42.7 0.0 copy-start.2
  42.7 2.3 %copy-done.2 = bf16[3072,768]{1,0:T(8,128)(2,1)S(1)} copy-done((bf16[3072,768]{1,0:T(8,128)(2,1)S(1)}, bf16[3072,768]{1,0:T(8,128)(2,1)}, u32[]{:S(2)}) %copy-start.2) | copy-done | bytes 4718616
  45.0 4.3 %weigh.1 = (f32[8,96,128]{2,1,0:T(8,128)}, f32[1,3072]{1,0:T(1,128)S(1)}) custom-call(f32[8,96,128]{2,1,0:T(8,128)S(1)} %all-to-all-done.1.unit_ref, bf16[3072,768]{1,0:T(8,128)(2,1)S(1)} %copy-done.2, f32[1,3072]{1,0:T(1,128)S(1)} %get-tuple-element.13.slot_ref, f32[1,3072]{1,0:T(1,128)S(1)} %lengths.1.length_ref), custom_call_target="tpu_custom_call" | custom-call | tf_op jit(solution)/shard_map/weigh/pallas_call | solution.py:229
  49.3 3.6 %all-to-all-start.2 = ((f32[8,96,128]{2,1,0:T(8,128)}), f32[8,96,128]{2,1,0:T(8,128)S(1)}, u32[]{:S(2)}, u32[]{:S(2)}) async-start(f32[8,96,128]{2,1,0:T(8,128)} %get-tuple-element.14), calls=%async_computation.2 | async-start | bytes 786432 | tf_op jit(solution)/shard_map/all_to_all | solution.py:201
  52.9 0.0 collective-permute-start
  52.9 1.6 %collective-permute-start.1 = (f32[3072]{0:T(1024)S(1)}, f32[3072]{0:T(1024)S(1)}, u32[]{:S(2)}, u32[]{:S(2)}) collective-permute-start(f32[3072]{0:T(1024)S(1)} %bitcast.5), channel_id=1, source_target_pairs={{0,2},{1,3},{2,0},{3,1},{4,6},{5,7},{6,4},{7,5},{8,10},{9,11},{10,... | collective-permute-start | bytes 36872 | tf_op jit(solution)/shard_map/ppermute | solution.py:241
  54.5 1.4 %collective-permute-start.2 = (f32[3072]{0:T(1024)S(1)}, f32[3072]{0:T(1024)S(1)}, u32[]{:S(2)}, u32[]{:S(2)}) collective-permute-start(f32[3072]{0:T(1024)S(1)} %bitcast.6), channel_id=1, source_target_pairs={{0,3},{1,0},{2,1},{3,2},{4,7},{5,4},{6,5},{7,6},{8,11},{9,8},{10,9... | collective-permute-start | bytes 36872 | tf_op jit(solution)/shard_map/ppermute | solution.py:241
  55.9 0.1 collective-permute-done
  56.1 0.6 collective-permute-done.1
  56.7 0.6 collective-permute-done.2
  57.3 0.6 add_add_fusion
  57.9 6.5 %all-to-all-done.2.got_ref = f32[8,96,128]{2,1,0:T(8,128)S(1)} async-done(((f32[8,96,128]{2,1,0:T(8,128)}), f32[8,96,128]{2,1,0:T(8,128)S(1)}, u32[]{:S(2)}, u32[]{:S(2)}) %all-to-all-start.2) | async-done | bytes 393248 | tf_op jit(solution)/shard_map/all_to_all | solution.py:201
  64.4 1.1 %prototypes.1 = f32[86,768]{1,0:T(8,128)} custom-call(f32[8,96,128]{2,1,0:T(8,128)S(1)} %all-to-all-done.2.got_ref, f32[1,128]{1,0:T(1,128)S(1)} %get-tuple-element.15.ids_ref), custom_call_target="tpu_custom_call" | custom-call | tf_op jit(solution)/shard_map/prototypes/pallas_call | solution.py:242
Async XLA Ops:
  1.4 2.3 %copy-start = (bf16[3072,768]{1,0:T(8,128)(2,1)S(1)}, bf16[3072,768]{1,0:T(8,128)(2,1)}, u32[]{:S(2)}) copy-start(bf16[3072,768]{1,0:T(8,128)(2,1)} %rows_ref.5) | copy-start | bytes 14155780
  3.7 0.7 %copy-start.3 = (s32[3072]{0:T(1024)S(1)}, s32[3072]{0:T(1024)}, u32[]{:S(2)}) copy-start(s32[3072]{0:T(1024)} %param.4) | copy-start | bytes 36868
  27.8 14.9 %all-to-all-start.1 = ((f32[8,96,128]{2,1,0:T(8,128)}), f32[8,96,128]{2,1,0:T(8,128)S(1)}, u32[]{:S(2)}, u32[]{:S(2)}) async-start(f32[8,96,128]{2,1,0:T(8,128)} %get-tuple-element.12), calls=%async_computation.1 | async-start | bytes 786432 | tf_op jit(solution)/shard_map/all_to_all | solution.py:201
  31.2 2.3 %copy-start.1 = (bf16[3072,768]{1,0:T(8,128)(2,1)S(1)}, bf16[3072,768]{1,0:T(8,128)(2,1)}, u32[]{:S(2)}) copy-start(bf16[3072,768]{1,0:T(8,128)(2,1)} %rows_ref.5) | copy-start | bytes 14155780
  42.7 2.3 %copy-start.2 = (bf16[3072,768]{1,0:T(8,128)(2,1)S(1)}, bf16[3072,768]{1,0:T(8,128)(2,1)}, u32[]{:S(2)}) copy-start(bf16[3072,768]{1,0:T(8,128)(2,1)} %rows_ref.5) | copy-start | bytes 14155780
  49.3 15.2 %all-to-all-start.2 = ((f32[8,96,128]{2,1,0:T(8,128)}), f32[8,96,128]{2,1,0:T(8,128)S(1)}, u32[]{:S(2)}, u32[]{:S(2)}) async-start(f32[8,96,128]{2,1,0:T(8,128)} %get-tuple-element.14), calls=%async_computation.2 | async-start | bytes 786432 | tf_op jit(solution)/shard_map/all_to_all | solution.py:201
  52.9 3.1 %collective-permute-start = (f32[3072]{0:T(1024)S(1)}, f32[3072]{0:T(1024)S(1)}, u32[]{:S(2)}, u32[]{:S(2)}) collective-permute-start(f32[3072]{0:T(1024)S(1)} %bitcast.4), channel_id=1, source_target_pairs={{0,1},{1,2},{2,3},{3,0},{4,5},{5,6},{6,7},{7,4},{8,9},{9,10},{10,1... | collective-permute-start | bytes 36872 | tf_op jit(solution)/shard_map/ppermute | solution.py:241
  52.9 3.8 %collective-permute-start.1 = (f32[3072]{0:T(1024)S(1)}, f32[3072]{0:T(1024)S(1)}, u32[]{:S(2)}, u32[]{:S(2)}) collective-permute-start(f32[3072]{0:T(1024)S(1)} %bitcast.5), channel_id=1, source_target_pairs={{0,2},{1,3},{2,0},{3,1},{4,6},{5,7},{6,4},{7,5},{8,10},{9,11},{10,... | collective-permute-start | bytes 36872 | tf_op jit(solution)/shard_map/ppermute | solution.py:241
  54.5 2.8 %collective-permute-start.2 = (f32[3072]{0:T(1024)S(1)}, f32[3072]{0:T(1024)S(1)}, u32[]{:S(2)}, u32[]{:S(2)}) collective-permute-start(f32[3072]{0:T(1024)S(1)} %bitcast.6), channel_id=1, source_target_pairs={{0,3},{1,0},{2,1},{3,2},{4,7},{5,4},{6,5},{7,6},{8,11},{9,8},{10,9... | collective-permute-start | bytes 36872 | tf_op jit(solution)/shard_map/ppermute | solution.py:241

commit v2 on v1

--- a/solution.py
+++ b/solution.py
@@ -17,7 +17,9 @@
 
 VMEM = pl.BlockSpec(memory_space=pltpu.VMEM)
 SMEM = pl.BlockSpec(memory_space=pltpu.SMEM)
+HBM = pl.BlockSpec(memory_space=pltpu.MemorySpace.HBM)
 VMEM_LIMIT = 24 * 1024 * 1024
+ROW_TILE = 512
 
 
 def dot(a, b, dims):
@@ -30,11 +32,9 @@
     return hi, lo
 
 
-def split3(x):
-    hi = x.astype(jnp.bfloat16)
-    rest = x - hi.astype(jnp.float32)
-    mid, lo = split2(rest)
-    return hi, mid, lo
+def pick(onehot, rows, axis):
+    both = jnp.concatenate([onehot, onehot], axis=axis)
+    return dot(both, jnp.concatenate(split2(rows), axis=0), ((axis,), (0,)))
 
 
 def flags(mask, dtype=jnp.bfloat16):
@@ -65,12 +65,26 @@
     return jnp.concatenate(rows, axis=0)
 
 
-def sums_kernel(group_count, place_ref, label_ref, rows_ref, out_ref, slot_ref):
+def fetch_rows(rows_hbm, rows_ref, row_sems, tile):
+    copies = []
+    for t in range(rows_ref.shape[0] // tile):
+        part = pl.ds(t * tile, tile)
+        copies.append(pltpu.make_async_copy(rows_hbm.at[part], rows_ref.at[part], row_sems.at[t]))
+        copies[-1].start()
+    return copies
+
+
+def sums_kernel(group_count, place_ref, label_hbm, rows_hbm, out_ref, slot_ref, label_ref, rows_ref, label_sem, row_sems):
     owner_count = out_ref.shape[0]
     slot_total = owner_count * SLOTS
     row_total, width = rows_ref.shape
     pieces = width // LANES
+    tile = min(ROW_TILE, row_total)
+    label_copy = pltpu.make_async_copy(label_hbm, label_ref, label_sem)
+    label_copy.start()
+    row_copies = fetch_rows(rows_hbm, rows_ref, row_sems, tile)
     my_group, my_owner, live = place_ref[0], place_ref[1], place_ref[2]
+    label_copy.wait()
     label = label_ref[...].astype(jnp.float32)
     block = jnp.floor((label + 0.5) * (1.0 / CLS_DEV))
     inner = label - block * CLS_DEV
@@ -91,8 +105,6 @@
     row_slot = jnp.sum(jnp.where(by_owner, row_slots, 0.0), axis=0, keepdims=True)
     where_to = jnp.where(owned, owner * SLOTS + row_slot, -1.0)
     slot_ref[...] = where_to
-    onehot = flags(iota((slot_total, row_total), 0) == where_to)
-    put_slots(out_ref, dot(onehot, rows_ref[...], ((1,), (0,))))
     class_at = iota((owner_pad, LANES), 1)
     lane = lax.broadcasted_iota(jnp.int32, (owner_pad, slot_total), 1) - my_owner * SLOTS
     ids = jnp.zeros((owner_pad, slot_total), jnp.float32)
@@ -107,9 +119,17 @@
     for o in range(owner_count):
         for t in range(slot_total // LANES):
             lanes = slice(t * LANES, (t + 1) * LANES)
-            tile = jnp.where(sub == 0, ids[o:o + 1, lanes], jnp.where(sub == 1, tally[o:o + 1, lanes], 0.0))
+            meta = jnp.where(sub == 0, ids[o:o + 1, lanes], jnp.where(sub == 1, tally[o:o + 1, lanes], 0.0))
             base = pieces * SLOTS + 8 * t
-            out_ref[o, base:base + 8, :] = tile
+            out_ref[o, base:base + 8, :] = meta
+    total = None
+    for t in range(row_total // tile):
+        part = slice(t * tile, (t + 1) * tile)
+        onehot = flags(iota((slot_total, tile), 0) == where_to[:, part])
+        row_copies[t].wait()
+        product = dot(onehot, rows_ref[part, :], ((1,), (0,)))
+        total = product if total is None else total + product
+    put_slots(out_ref, total)
 
 
 def means_kernel(got_ref, means_ref, back_ref, ids_ref):
@@ -130,11 +150,11 @@
     match = iota((CLS_PAD, slot_total), 0) == ids
     counts = jnp.sum(jnp.where(match, meta[1:2, :], 0.0), axis=1, keepdims=True)
     onehot = flags(match)
-    sums = sum(dot(onehot, part, ((1,), (0,))) for part in split3(get_slots(got_ref, pieces)))
-    means = sums / jnp.maximum(counts, 1.0)
+    sums = pick(onehot, get_slots(got_ref, pieces), 1)
+    means = sums * (1.0 / jnp.maximum(counts, 1.0))
     means_ref[...] = means[:means_ref.shape[0]]
-    unit = means / jnp.sqrt(jnp.sum(means * means, axis=1, keepdims=True) + epsilon)
-    put_slots(back_ref, sum(dot(onehot, part, ((0,), (0,))) for part in split2(unit)))
+    unit = means * (1.0 / jnp.sqrt(jnp.sum(means * means, axis=1, keepdims=True) + epsilon))
+    put_slots(back_ref, pick(onehot, unit, 0))
 
 
 def lengths_kernel(rows_ref, out_ref):
@@ -148,39 +168,33 @@
         out_ref[:, t * tile:(t + 1) * tile] = jnp.sqrt(total[0:1] + epsilon)
 
 
-def weigh_kernel(unit_ref, rows_ref, slot_ref, length_ref, out_ref, sim_ref, acc_ref):
+def weigh_kernel(unit_ref, rows_hbm, slot_ref, length_ref, out_ref, sim_ref, weight_ref, rows_ref, row_sems):
     row_total, width = rows_ref.shape
+    tile = min(ROW_TILE, row_total)
+    row_copies = fetch_rows(rows_hbm, rows_ref, row_sems, tile)
     slot_total = out_ref.shape[0] * SLOTS
     units = jnp.concatenate(split2(get_slots(unit_ref, width // LANES)), axis=0)
-    tile = min(512, row_total)
     for t in range(row_total // tile):
         part = slice(t * tile, (t + 1) * tile)
-        rows = rows_ref[part, :]
-        products = dot(units, rows, ((1,), (1,)))
+        row_copies[t].wait()
+        products = dot(units, rows_ref[part, :], ((1,), (1,)))
         where_to = slot_ref[:, part]
         hit = iota((slot_total, tile), 0) == where_to
         product = jnp.sum(
             jnp.where(hit, products[:slot_total] + products[slot_total:], 0.0), axis=0, keepdims=True
         )
-        owned = where_to >= 0
-        similarity = jnp.where(owned, product / length_ref[:, part], 0.0)
+        similarity = jnp.where(where_to >= 0, product / length_ref[:, part], 0.0)
         sim_ref[:, part] = similarity
         weight = jnp.exp(sharpness * (similarity - 1.0))
-        weights = jnp.where(hit, weight, 0.0).astype(jnp.bfloat16)
-        weighted = dot(weights, rows, ((1,), (0,)))
-        if t == 0:
-            acc_ref[...] = weighted
-        else:
-            acc_ref[...] += weighted
-    put_slots(out_ref, acc_ref[...])
+        weight_ref[:, part] = jnp.where(hit, weight, 0.0).astype(jnp.bfloat16)
+    put_slots(out_ref, dot(weight_ref[...], rows_ref[...], ((1,), (0,))))
 
 
 def prototypes_kernel(got_ref, ids_ref, out_ref):
     slot_total = got_ref.shape[0] * SLOTS
     onehot = flags(iota((CLS_PAD, slot_total), 0) == ids_ref[...])
-    rows = get_slots(got_ref, out_ref.shape[1] // LANES)
-    weighted = sum(dot(onehot, part, ((1,), (0,))) for part in split3(rows))
-    unit = weighted / jnp.sqrt(jnp.sum(weighted * weighted, axis=1, keepdims=True) + epsilon)
+    weighted = pick(onehot, get_slots(got_ref, out_ref.shape[1] // LANES), 1)
+    unit = weighted * (1.0 / jnp.sqrt(jnp.sum(weighted * weighted, axis=1, keepdims=True) + epsilon))
     out_ref[...] = unit[:out_ref.shape[0]]
 
 
@@ -189,12 +203,19 @@
         kernel,
         in_specs=ins,
         out_specs=[VMEM] * len(outs),
-        out_shape=[jax.ShapeDtypeStruct(shape, jnp.float32) for shape in outs],
+        out_shape=[
+            shape if isinstance(shape, jax.ShapeDtypeStruct) else jax.ShapeDtypeStruct(shape, jnp.float32)
+            for shape in outs
+        ],
         scratch_shapes=list(scratch),
         compiler_params=pltpu.CompilerParams(vmem_limit_bytes=VMEM_LIMIT),
         cost_estimate=cost,
         name=name,
     )
+
+
+def in_hbm(array):
+    return pltpu.with_memory_space_constraint(array, pltpu.MemorySpace.HBM)
 
 
 def exchange(payload):
@@ -208,14 +229,24 @@
     slot_total = owner_count * SLOTS
     pieces = width // LANES
     slot_rows = pieces * SLOTS
+    tiles = row_total // min(ROW_TILE, row_total)
     meta_rows = 8 * (slot_total // LANES)
     place = jnp.stack([lax.axis_index("cls"), lax.axis_index("dp"), row_count[0]]).astype(jnp.int32)
     payload, where_to = call(
         functools.partial(sums_kernel, group_count),
-        [SMEM, VMEM, VMEM],
-        [(owner_count, slot_rows + meta_rows, LANES), (1, row_total)],
+        [SMEM, HBM, HBM],
+        [
+            (owner_count, slot_rows + meta_rows, LANES),
+            (1, row_total),
+        ],
         "sums",
-    )(place, labels.reshape(1, row_total), embeddings)
+        scratch=[
+            pltpu.VMEM((1, row_total), jnp.int32),
+            pltpu.VMEM((row_total, width), jnp.bfloat16),
+            pltpu.SemaphoreType.DMA,
+            pltpu.SemaphoreType.DMA((tiles,)),
+        ],
+    )(place, in_hbm(labels.reshape(1, row_total)), in_hbm(embeddings))
     got = exchange(payload)
     cost = pl.CostEstimate(flops=8 * row_total * width * 128, bytes_accessed=2 * row_total * width, transcendentals=row_total)
     (lengths,) = call(lengths_kernel, [VMEM], [(1, row_total)], "lengths", cost=cost)(embeddings)
@@ -228,11 +259,15 @@
     units = exchange(back)
     weighted, own_similarity = call(
         weigh_kernel,
-        [VMEM] * 4,
+        [VMEM, HBM, VMEM, VMEM],
         [(owner_count, slot_rows, LANES), (1, row_total)],
         "weigh",
-        scratch=[pltpu.VMEM((slot_total, width), jnp.float32)],
-    )(units, embeddings, where_to, lengths)
+        scratch=[
+            pltpu.VMEM((slot_total, row_total), jnp.bfloat16),
+            pltpu.VMEM((row_total, width), jnp.bfloat16),
+            pltpu.SemaphoreType.DMA((tiles,)),
+        ],
+    )(units, in_hbm(embeddings), where_to, lengths)
     got_weighted = exchange(weighted)
     own = own_similarity.reshape(row_total)
     similarity = own

time: 66.1 us -> 64.4 us (0.974)
  local copies, waits for them, and re-layouts: 7.71 us -> 2.33 us
  Pallas kernels: 11.7 us -> 15.6 us
    unnamed x8 -> x2, local copies, waits for them, and re-layouts: 7.71 us -> 2.33 us
    pallas_call x2, Pallas kernels: 6.51 us -> 10.6 us  [the longest x1 5.45 us: shards(): call(weigh_kernel, [VMEM, HBM, VMEM, VMEM], [(owner_count, slot_rows, LAN...]
where the time goes in v2:
time: 64.4 us; the launch traced here: 64 us
  blocking collectives  19.7 us (31%)
  Pallas kernels  15.6 us (24%)
  waiting for transfers between devices  14.3 us (22%)
  starting transfers between devices  10.1 us (16%)
  local copies, waits for them, and re-layouts  2.33 us (4%)
  between operations  1.33 us (2%)
  other arithmetic  0.68 us (1%)
    all_to_all x1, blocking collectives, exchange(): lax.all_to_all(payload, 'dp', split_axis=0, concat_axis=0, tiled=True)  19.7 us
    all_to_all x2, waiting for transfers between devices, exchange(): lax.all_to_all(payload, 'dp', split_axis=0, concat_axis=0, tiled=True)  12.9 us
    all_to_all x2, starting transfers between devices, exchange(): lax.all_to_all(payload, 'dp', split_axis=0, concat_axis=0, tiled=True)  7.11 us
    pallas_call x1, Pallas kernels, shards(): call(weigh_kernel, [VMEM, HBM, VMEM, VMEM], [(owner_count, slot_rows, LAN...  5.45 us
    pallas_call x1, Pallas kernels, shards(): call(functools.partial(sums_kernel, group_count), [SMEM, HBM, HBM], [(own...  5.16 us
    ppermute x3, starting transfers between devices, shards(): similarity = similarity + lax.ppermute(own, 'cls', ring)  2.99 us
    pallas_call x1, Pallas kernels, shards(): call(lengths_kernel, [VMEM], [(1, row_total)], 'lengths', cost=cost)  2.65 us
    unnamed x2, local copies, waits for them, and re-layouts  2.33 us
  transfers between devices with their start and end apart: 5, of which 5 were waited for; matrix products, arithmetic and copies ran while one was open for 1% of the time, Pallas kernels for 4%

profile of v2, /device:TPU:0, one launch (start us, length us, event | category | flops | bytes accessed | tf_op | source)
XLA Modules:
  0.0 64.0 jit_solution(8436477370096950845)
XLA Ops:
  1.3 0.1 pad_add_fusion.place_ref
  1.4 5.2 %sums.1 = (f32[8,104,128]{2,1,0:T(8,128)S(1)}, f32[1,3072]{1,0:T(1,128)S(1)}) custom-call(s32[3]{0:T(128)S(1)} %pad_add_fusion.place_ref, s32[1,3072]{1,0:T(1,128)} %bitcast.8, bf16[3072,768]{1,0:T(8,128)(2,1)} %rows_hbm.3), custom_call_target="tpu_custom_call" | custom-call | tf_op jit(solution)/shard_map/sums/pallas_call | solution.py:235
  6.5 19.7 %all_to_all.15.got_ref = f32[8,104,128]{2,1,0:T(8,128)S(1)} all-to-all(f32[8,104,128]{2,1,0:T(8,128)S(1)} %get-tuple-element.10), channel_id=1, replica_groups=mesh['dp'=8,'cls'=4] {'dp'}, dimensions={0} | all-to-all | bytes 851968 | tf_op jit(solution)/shard_map/all_to_all | solution.py:222
  26.2 1.3 %means.1 = (f32[86,768]{1,0:T(8,128)}, f32[8,96,128]{2,1,0:T(8,128)}, f32[1,128]{1,0:T(1,128)S(1)}) custom-call(f32[8,104,128]{2,1,0:T(8,128)S(1)} %all_to_all.15.got_ref), custom_call_target="tpu_custom_call" | custom-call | tf_op jit(solution)/shard_map/means/pallas_call | solution.py:253
  27.5 3.5 %all-to-all-start.1 = ((f32[8,96,128]{2,1,0:T(8,128)}), f32[8,96,128]{2,1,0:T(8,128)S(1)}, u32[]{:S(2)}, u32[]{:S(2)}) async-start(f32[8,96,128]{2,1,0:T(8,128)} %get-tuple-element.12), calls=%async_computation.1 | async-start | bytes 786432 | tf_op jit(solution)/shard_map/all_to_all | solution.py:222
  31.0 0.0 copy-start
  31.0 2.3 %copy-done = bf16[3072,768]{1,0:T(8,128)(2,1)S(1)} copy-done((bf16[3072,768]{1,0:T(8,128)(2,1)S(1)}, bf16[3072,768]{1,0:T(8,128)(2,1)}, u32[]{:S(2)}) %copy-start) | copy-done | bytes 4718616
  33.3 2.7 %lengths.1.length_ref = f32[1,3072]{1,0:T(1,128)S(1)} custom-call(bf16[3072,768]{1,0:T(8,128)(2,1)S(1)} %copy-done), custom_call_target="tpu_custom_call" | custom-call | flops 2415919104 | bytes 4718592 | tf_op jit(solution)/shard_map/lengths/pallas_call | solution.py:252
  36.0 6.4 %all-to-all-done.1.unit_ref = f32[8,96,128]{2,1,0:T(8,128)S(1)} async-done(((f32[8,96,128]{2,1,0:T(8,128)}), f32[8,96,128]{2,1,0:T(8,128)S(1)}, u32[]{:S(2)}, u32[]{:S(2)}) %all-to-all-start.1) | async-done | bytes 393248 | tf_op jit(solution)/shard_map/all_to_all | solution.py:222
  42.4 5.5 %weigh.1 = (f32[8,96,128]{2,1,0:T(8,128)}, f32[1,3072]{1,0:T(1,128)S(1)}) custom-call(f32[8,96,128]{2,1,0:T(8,128)S(1)} %all-to-all-done.1.unit_ref, bf16[3072,768]{1,0:T(8,128)(2,1)} %rows_hbm.3, f32[1,3072]{1,0:T(1,128)S(1)} %get-tuple-element.13.slot_ref, f32[1,3072]{1,0:T(1,128)S(1)} %lengths.1.length_ref), custom_call_target="tpu_custom_call" | custom-call | tf_op jit(solution)/shard_map/weigh/pallas_call | solution.py:260
  47.9 3.7 %all-to-all-start.2 = ((f32[8,96,128]{2,1,0:T(8,128)}), f32[8,96,128]{2,1,0:T(8,128)S(1)}, u32[]{:S(2)}, u32[]{:S(2)}) async-start(f32[8,96,128]{2,1,0:T(8,128)} %get-tuple-element.14), calls=%async_computation.2 | async-start | bytes 786432 | tf_op jit(solution)/shard_map/all_to_all | solution.py:222
  51.5 0.0 collective-permute-start
  51.5 1.6 %collective-permute-start.1 = (f32[3072]{0:T(1024)S(1)}, f32[3072]{0:T(1024)S(1)}, u32[]{:S(2)}, u32[]{:S(2)}) collective-permute-start(f32[3072]{0:T(1024)S(1)} %bitcast.5), channel_id=1, source_target_pairs={{0,2},{1,3},{2,0},{3,1},{4,6},{5,7},{6,4},{7,5},{8,10},{9,11},{10,... | collective-permute-start | bytes 36872 | tf_op jit(solution)/shard_map/ppermute | solution.py:276
  53.1 1.4 %collective-permute-start.2 = (f32[3072]{0:T(1024)S(1)}, f32[3072]{0:T(1024)S(1)}, u32[]{:S(2)}, u32[]{:S(2)}) collective-permute-start(f32[3072]{0:T(1024)S(1)} %bitcast.6), channel_id=1, source_target_pairs={{0,3},{1,0},{2,1},{3,2},{4,7},{5,4},{6,5},{7,6},{8,11},{9,8},{10,9... | collective-permute-start | bytes 36872 | tf_op jit(solution)/shard_map/ppermute | solution.py:276
  54.5 0.1 collective-permute-done
  54.6 0.6 %collective-permute-done.1 = f32[3072]{0:T(1024)S(1)} collective-permute-done((f32[3072]{0:T(1024)S(1)}, f32[3072]{0:T(1024)S(1)}, u32[]{:S(2)}, u32[]{:S(2)}) %collective-permute-start.1) | collective-permute-done | bytes 12320 | tf_op jit(solution)/shard_map/ppermute | solution.py:276
  55.3 0.6 collective-permute-done.2
  55.9 0.6 add_add_fusion
  56.5 6.5 %all-to-all-done.2.got_ref = f32[8,96,128]{2,1,0:T(8,128)S(1)} async-done(((f32[8,96,128]{2,1,0:T(8,128)}), f32[8,96,128]{2,1,0:T(8,128)S(1)}, u32[]{:S(2)}, u32[]{:S(2)}) %all-to-all-start.2) | async-done | bytes 393248 | tf_op jit(solution)/shard_map/all_to_all | solution.py:222
  63.0 1.0 %prototypes.1 = f32[86,768]{1,0:T(8,128)} custom-call(f32[8,96,128]{2,1,0:T(8,128)S(1)} %all-to-all-done.2.got_ref, f32[1,128]{1,0:T(1,128)S(1)} %get-tuple-element.15.ids_ref), custom_call_target="tpu_custom_call" | custom-call | tf_op jit(solution)/shard_map/prototypes/pallas_call | solution.py:277
Async XLA Ops:
  27.5 14.9 %all-to-all-start.1 = ((f32[8,96,128]{2,1,0:T(8,128)}), f32[8,96,128]{2,1,0:T(8,128)S(1)}, u32[]{:S(2)}, u32[]{:S(2)}) async-start(f32[8,96,128]{2,1,0:T(8,128)} %get-tuple-element.12), calls=%async_computation.1 | async-start | bytes 786432 | tf_op jit(solution)/shard_map/all_to_all | solution.py:222
  31.0 2.3 %copy-start = (bf16[3072,768]{1,0:T(8,128)(2,1)S(1)}, bf16[3072,768]{1,0:T(8,128)(2,1)}, u32[]{:S(2)}) copy-start(bf16[3072,768]{1,0:T(8,128)(2,1)} %rows_hbm.3) | copy-start | bytes 14155780
  47.9 15.2 %all-to-all-start.2 = ((f32[8,96,128]{2,1,0:T(8,128)}), f32[8,96,128]{2,1,0:T(8,128)S(1)}, u32[]{:S(2)}, u32[]{:S(2)}) async-start(f32[8,96,128]{2,1,0:T(8,128)} %get-tuple-element.14), calls=%async_computation.2 | async-start | bytes 786432 | tf_op jit(solution)/shard_map/all_to_all | solution.py:222
  51.5 3.1 %collective-permute-start = (f32[3072]{0:T(1024)S(1)}, f32[3072]{0:T(1024)S(1)}, u32[]{:S(2)}, u32[]{:S(2)}) collective-permute-start(f32[3072]{0:T(1024)S(1)} %bitcast.4), channel_id=1, source_target_pairs={{0,1},{1,2},{2,3},{3,0},{4,5},{5,6},{6,7},{7,4},{8,9},{9,10},{10,1... | collective-permute-start | bytes 36872 | tf_op jit(solution)/shard_map/ppermute | solution.py:276
  51.5 3.8 %collective-permute-start.1 = (f32[3072]{0:T(1024)S(1)}, f32[3072]{0:T(1024)S(1)}, u32[]{:S(2)}, u32[]{:S(2)}) collective-permute-start(f32[3072]{0:T(1024)S(1)} %bitcast.5), channel_id=1, source_target_pairs={{0,2},{1,3},{2,0},{3,1},{4,6},{5,7},{6,4},{7,5},{8,10},{9,11},{10,... | collective-permute-start | bytes 36872 | tf_op jit(solution)/shard_map/ppermute | solution.py:276
  53.1 2.8 %collective-permute-start.2 = (f32[3072]{0:T(1024)S(1)}, f32[3072]{0:T(1024)S(1)}, u32[]{:S(2)}, u32[]{:S(2)}) collective-permute-start(f32[3072]{0:T(1024)S(1)} %bitcast.6), channel_id=1, source_target_pairs={{0,3},{1,0},{2,1},{3,2},{4,7},{5,4},{6,5},{7,6},{8,11},{9,8},{10,9... | collective-permute-start | bytes 36872 | tf_op jit(solution)/shard_map/ppermute | solution.py:276

commit v3 on v2

--- a/solution.py
+++ b/solution.py
@@ -19,7 +19,6 @@
 SMEM = pl.BlockSpec(memory_space=pltpu.SMEM)
 HBM = pl.BlockSpec(memory_space=pltpu.MemorySpace.HBM)
 VMEM_LIMIT = 24 * 1024 * 1024
-ROW_TILE = 512
 
 
 def dot(a, b, dims):
@@ -65,10 +64,15 @@
     return jnp.concatenate(rows, axis=0)
 
 
-def fetch_rows(rows_hbm, rows_ref, row_sems, tile):
+def row_cuts(row_total):
+    first = row_total * 2 // 3 // LANES * LANES
+    return [0, first, row_total] if first else [0, row_total]
+
+
+def fetch_rows(rows_hbm, rows_ref, row_sems, cuts):
     copies = []
-    for t in range(rows_ref.shape[0] // tile):
-        part = pl.ds(t * tile, tile)
+    for t in range(len(cuts) - 1):
+        part = pl.ds(cuts[t], cuts[t + 1] - cuts[t])
         copies.append(pltpu.make_async_copy(rows_hbm.at[part], rows_ref.at[part], row_sems.at[t]))
         copies[-1].start()
     return copies
@@ -79,10 +83,10 @@
     slot_total = owner_count * SLOTS
     row_total, width = rows_ref.shape
     pieces = width // LANES
-    tile = min(ROW_TILE, row_total)
+    cuts = row_cuts(row_total)
     label_copy = pltpu.make_async_copy(label_hbm, label_ref, label_sem)
     label_copy.start()
-    row_copies = fetch_rows(rows_hbm, rows_ref, row_sems, tile)
+    row_copies = fetch_rows(rows_hbm, rows_ref, row_sems, cuts)
     my_group, my_owner, live = place_ref[0], place_ref[1], place_ref[2]
     label_copy.wait()
     label = label_ref[...].astype(jnp.float32)
@@ -123,9 +127,9 @@
             base = pieces * SLOTS + 8 * t
             out_ref[o, base:base + 8, :] = meta
     total = None
-    for t in range(row_total // tile):
-        part = slice(t * tile, (t + 1) * tile)
-        onehot = flags(iota((slot_total, tile), 0) == where_to[:, part])
+    for t in range(len(cuts) - 1):
+        part = slice(cuts[t], cuts[t + 1])
+        onehot = flags(iota((slot_total, cuts[t + 1] - cuts[t]), 0) == where_to[:, part])
         row_copies[t].wait()
         product = dot(onehot, rows_ref[part, :], ((1,), (0,)))
         total = product if total is None else total + product
@@ -157,10 +161,11 @@
     put_slots(back_ref, pick(onehot, unit, 0))
 
 
-def lengths_kernel(rows_ref, out_ref):
+def lengths_kernel(rows_ref, out_ref, head_ref):
     row_total, width = rows_ref.shape
     tile = min(512, row_total)
     ones = jnp.ones((16, width), jnp.bfloat16)
+    head_ref[...] = rows_ref[:head_ref.shape[0], :]
     for t in range(row_total // tile):
         features = rows_ref[t * tile:(t + 1) * tile, :].astype(jnp.float32)
         hi, lo = split2(features * features)
@@ -168,18 +173,20 @@
         out_ref[:, t * tile:(t + 1) * tile] = jnp.sqrt(total[0:1] + epsilon)
 
 
-def weigh_kernel(unit_ref, rows_hbm, slot_ref, length_ref, out_ref, sim_ref, weight_ref, rows_ref, row_sems):
-    row_total, width = rows_ref.shape
-    tile = min(ROW_TILE, row_total)
-    row_copies = fetch_rows(rows_hbm, rows_ref, row_sems, tile)
+def weigh_kernel(unit_ref, head_ref, rows_hbm, slot_ref, length_ref, out_ref, sim_ref, weight_ref, tail_ref, tail_sem):
+    head_total, width = head_ref.shape
     slot_total = out_ref.shape[0] * SLOTS
+    tail_copy = pltpu.make_async_copy(rows_hbm.at[pl.ds(head_total, tail_ref.shape[0])], tail_ref, tail_sem)
+    tail_copy.start()
     units = jnp.concatenate(split2(get_slots(unit_ref, width // LANES)), axis=0)
-    for t in range(row_total // tile):
-        part = slice(t * tile, (t + 1) * tile)
-        row_copies[t].wait()
-        products = dot(units, rows_ref[part, :], ((1,), (1,)))
+    total = None
+    for rows_ref, first in ((head_ref, 0), (tail_ref, head_total)):
+        part = slice(first, first + rows_ref.shape[0])
         where_to = slot_ref[:, part]
-        hit = iota((slot_total, tile), 0) == where_to
+        hit = iota((slot_total, rows_ref.shape[0]), 0) == where_to
+        if first:
+            tail_copy.wait()
+        products = dot(units, rows_ref[...], ((1,), (1,)))
         product = jnp.sum(
             jnp.where(hit, products[:slot_total] + products[slot_total:], 0.0), axis=0, keepdims=True
         )
@@ -187,7 +194,9 @@
         sim_ref[:, part] = similarity
         weight = jnp.exp(sharpness * (similarity - 1.0))
         weight_ref[:, part] = jnp.where(hit, weight, 0.0).astype(jnp.bfloat16)
-    put_slots(out_ref, dot(weight_ref[...], rows_ref[...], ((1,), (0,))))
+        weighted = dot(weight_ref[:, part], rows_ref[...], ((1,), (0,)))
+        total = weighted if total is None else total + weighted
+    put_slots(out_ref, total)
 
 
 def prototypes_kernel(got_ref, ids_ref, out_ref):
@@ -229,7 +238,6 @@
     slot_total = owner_count * SLOTS
     pieces = width // LANES
     slot_rows = pieces * SLOTS
-    tiles = row_total // min(ROW_TILE, row_total)
     meta_rows = 8 * (slot_total // LANES)
     place = jnp.stack([lax.axis_index("cls"), lax.axis_index("dp"), row_count[0]]).astype(jnp.int32)
     payload, where_to = call(
@@ -244,12 +252,19 @@
             pltpu.VMEM((1, row_total), jnp.int32),
             pltpu.VMEM((row_total, width), jnp.bfloat16),
             pltpu.SemaphoreType.DMA,
-            pltpu.SemaphoreType.DMA((tiles,)),
+            pltpu.SemaphoreType.DMA((len(row_cuts(row_total)) - 1,)),
         ],
     )(place, in_hbm(labels.reshape(1, row_total)), in_hbm(embeddings))
     got = exchange(payload)
     cost = pl.CostEstimate(flops=8 * row_total * width * 128, bytes_accessed=2 * row_total * width, transcendentals=row_total)
-    (lengths,) = call(lengths_kernel, [VMEM], [(1, row_total)], "lengths", cost=cost)(embeddings)
+    head = row_total // 2
+    lengths, head_rows = call(
+        lengths_kernel,
+        [VMEM],
+        [(1, row_total), jax.ShapeDtypeStruct((head, width), jnp.bfloat16)],
+        "lengths",
+        cost=cost,
+    )(embeddings)
     class_means, back, ids = call(
         means_kernel,
         [VMEM],
@@ -259,15 +274,15 @@
     units = exchange(back)
     weighted, own_similarity = call(
         weigh_kernel,
-        [VMEM, HBM, VMEM, VMEM],
+        [VMEM, VMEM, HBM, VMEM, VMEM],
         [(owner_count, slot_rows, LANES), (1, row_total)],
         "weigh",
         scratch=[
             pltpu.VMEM((slot_total, row_total), jnp.bfloat16),
-            pltpu.VMEM((row_total, width), jnp.bfloat16),
-            pltpu.SemaphoreType.DMA((tiles,)),
-        ],
-    )(units, in_hbm(embeddings), where_to, lengths)
+            pltpu.VMEM((row_total - head, width), jnp.bfloat16),
+            pltpu.SemaphoreType.DMA,
+        ],
+    )(units, head_rows, in_hbm(embeddings), where_to, lengths)
     got_weighted = exchange(weighted)
     own = own_similarity.reshape(row_total)
     similarity = own

time: 64.4 us -> 62.3 us (0.967)
  Pallas kernels: 15.6 us -> 13.6 us
  starting transfers between devices: 10.1 us -> 8.86 us
  waiting for transfers between devices: 14.3 us -> 15.4 us
    ppermute x3, waiting for transfers between devices: 1.4 us -> 2.96 us  [shards(): similarity = similarity + lax.ppermute(own, 'cls', ring)]
    ppermute x3, starting transfers between devices: 2.99 us -> 1.75 us  [shards(): similarity = similarity + lax.ppermute(own, 'cls', ring)]
    pallas_call x2, Pallas kernels: 8.11 us -> 6.98 us  [the longest x1 4.18 us: shards(): call(weigh_kernel, [VMEM, VMEM, HBM, VMEM, VMEM], [(owner_count, slot_row...]
    pallas_call x1, Pallas kernels: 5.16 us -> 4.31 us  [shards(): call(functools.partial(sums_kernel, group_count), [SMEM, HBM, HBM], [(own...]
  transfers between devices with their start and end apart: 5 -> 5, of which waited for: 5 -> 5; matrix products, arithmetic and copies ran while one was open for 1% -> 1% of each run, Pallas kernels for 4% -> 5%
where the time goes in v3:
time: 62.3 us; the launch traced here: 61.9 us
  blocking collectives  19.7 us (32%)
  waiting for transfers between devices  15.4 us (25%)
  Pallas kernels  13.6 us (22%)
  starting transfers between devices  8.86 us (14%)
  local copies, waits for them, and re-layouts  2.33 us (4%)
  between operations  1.33 us (2%)
  other arithmetic  0.68 us (1%)
    all_to_all x1, blocking collectives, exchange(): lax.all_to_all(payload, 'dp', split_axis=0, concat_axis=0, tiled=True)  19.7 us
    all_to_all x2, waiting for transfers between devices, exchange(): lax.all_to_all(payload, 'dp', split_axis=0, concat_axis=0, tiled=True)  12.5 us
    all_to_all x2, starting transfers between devices, exchange(): lax.all_to_all(payload, 'dp', split_axis=0, concat_axis=0, tiled=True)  7.11 us
    pallas_call x1, Pallas kernels, shards(): call(functools.partial(sums_kernel, group_count), [SMEM, HBM, HBM], [(own...  4.31 us
    pallas_call x1, Pallas kernels, shards(): call(weigh_kernel, [VMEM, VMEM, HBM, VMEM, VMEM], [(owner_count, slot_row...  4.18 us
    ppermute x3, waiting for transfers between devices, shards(): similarity = similarity + lax.ppermute(own, 'cls', ring)  2.96 us
    pallas_call x1, Pallas kernels, shards(): call(lengths_kernel, [VMEM], [(1, row_total), jax.ShapeDtypeStruct((head,...  2.8 us
    unnamed x2, local copies, waits for them, and re-layouts  2.33 us
  transfers between devices with their start and end apart: 5, of which 5 were waited for; matrix products, arithmetic and copies ran while one was open for 1% of the time, Pallas kernels for 5%

profile of v3, /device:TPU:0, one launch (start us, length us, event | category | flops | bytes accessed | tf_op | source)
XLA Modules:
  0.0 61.9 jit_solution(16603628868420164415)
XLA Ops:
  1.3 0.1 pad_add_fusion.place_ref
  1.4 4.3 %sums.1 = (f32[8,104,128]{2,1,0:T(8,128)S(1)}, f32[1,3072]{1,0:T(1,128)S(1)}) custom-call(s32[3]{0:T(128)S(1)} %pad_add_fusion.place_ref, s32[1,3072]{1,0:T(1,128)} %bitcast.8, bf16[3072,768]{1,0:T(8,128)(2,1)} %rows_hbm.3), custom_call_target="tpu_custom_call" | custom-call | tf_op jit(solution)/shard_map/sums/pallas_call | solution.py:243
  5.7 19.7 %all_to_all.15.got_ref = f32[8,104,128]{2,1,0:T(8,128)S(1)} all-to-all(f32[8,104,128]{2,1,0:T(8,128)S(1)} %get-tuple-element.12), channel_id=1, replica_groups=mesh['dp'=8,'cls'=4] {'dp'}, dimensions={0} | all-to-all | bytes 851968 | tf_op jit(solution)/shard_map/all_to_all | solution.py:231
  25.4 1.3 %means.1 = (f32[86,768]{1,0:T(8,128)}, f32[8,96,128]{2,1,0:T(8,128)}, f32[1,128]{1,0:T(1,128)S(1)}) custom-call(f32[8,104,128]{2,1,0:T(8,128)S(1)} %all_to_all.15.got_ref), custom_call_target="tpu_custom_call" | custom-call | tf_op jit(solution)/shard_map/means/pallas_call | solution.py:268
  26.6 3.5 %all-to-all-start.1 = ((f32[8,96,128]{2,1,0:T(8,128)}), f32[8,96,128]{2,1,0:T(8,128)S(1)}, u32[]{:S(2)}, u32[]{:S(2)}) async-start(f32[8,96,128]{2,1,0:T(8,128)} %get-tuple-element.14), calls=%async_computation.1 | async-start | bytes 786432 | tf_op jit(solution)/shard_map/all_to_all | solution.py:231
  30.1 0.0 copy-start
  30.1 2.3 %copy-done = bf16[3072,768]{1,0:T(8,128)(2,1)S(1)} copy-done((bf16[3072,768]{1,0:T(8,128)(2,1)S(1)}, bf16[3072,768]{1,0:T(8,128)(2,1)}, u32[]{:S(2)}) %copy-start) | copy-done | bytes 4718616
  32.4 2.8 %lengths.1 = (f32[1,3072]{1,0:T(1,128)S(1)}, bf16[1536,768]{1,0:T(8,128)(2,1)S(1)}) custom-call(bf16[3072,768]{1,0:T(8,128)(2,1)S(1)} %copy-done), custom_call_target="tpu_custom_call" | custom-call | flops 2415919104 | bytes 4718592 | tf_op jit(solution)/shard_map/lengths/pallas_call | solution.py:261
  35.3 6.3 %all-to-all-done.1.unit_ref = f32[8,96,128]{2,1,0:T(8,128)S(1)} async-done(((f32[8,96,128]{2,1,0:T(8,128)}), f32[8,96,128]{2,1,0:T(8,128)S(1)}, u32[]{:S(2)}, u32[]{:S(2)}) %all-to-all-start.1) | async-done | bytes 393248 | tf_op jit(solution)/shard_map/all_to_all | solution.py:231
  41.5 4.2 %weigh.1 = (f32[8,96,128]{2,1,0:T(8,128)}, f32[1,3072]{1,0:T(1,128)S(1)}) custom-call(f32[8,96,128]{2,1,0:T(8,128)S(1)} %all-to-all-done.1.unit_ref, bf16[1536,768]{1,0:T(8,128)(2,1)S(1)} %get-tuple-element.15.head_ref, bf16[3072,768]{1,0:T(8,128)(2,1)} %rows_hbm.3, f32[1,3072]{1,0:T(1,128)S(1)} %get-tuple-element.16.slot_ref, ...), custom_call_target="tpu_custom_call" | custom-call | tf_op jit(solution)/shard_map/weigh/pallas_call | solution.py:275
  45.7 3.7 %all-to-all-start.2 = ((f32[8,96,128]{2,1,0:T(8,128)}), f32[8,96,128]{2,1,0:T(8,128)S(1)}, u32[]{:S(2)}, u32[]{:S(2)}) async-start(f32[8,96,128]{2,1,0:T(8,128)} %get-tuple-element.18), calls=%async_computation.2 | async-start | bytes 786432 | tf_op jit(solution)/shard_map/all_to_all | solution.py:231
  49.4 0.5 collective-permute-start.2
  49.8 1.1 %collective-permute-start.1 = (f32[3072]{0:T(1024)S(1)}, f32[3072]{0:T(1024)S(1)}, u32[]{:S(2)}, u32[]{:S(2)}) collective-permute-start(f32[3072]{0:T(1024)S(1)} %bitcast.5), channel_id=1, source_target_pairs={{0,2},{1,3},{2,0},{3,1},{4,6},{5,7},{6,4},{7,5},{8,10},{9,11},{10,... | collective-permute-start | bytes 36872 | tf_op jit(solution)/shard_map/ppermute | solution.py:291
  51.0 0.2 collective-permute-start
  51.1 0.1 collective-permute-done.2
  51.3 2.3 %collective-permute-done.1 = f32[3072]{0:T(1024)S(1)} collective-permute-done((f32[3072]{0:T(1024)S(1)}, f32[3072]{0:T(1024)S(1)}, u32[]{:S(2)}, u32[]{:S(2)}) %collective-permute-start.1) | collective-permute-done | bytes 12320 | tf_op jit(solution)/shard_map/ppermute | solution.py:291
  53.5 0.6 collective-permute-done
  54.1 0.6 add_add_fusion
  54.7 6.2 %all-to-all-done.2.got_ref = f32[8,96,128]{2,1,0:T(8,128)S(1)} async-done(((f32[8,96,128]{2,1,0:T(8,128)}), f32[8,96,128]{2,1,0:T(8,128)S(1)}, u32[]{:S(2)}, u32[]{:S(2)}) %all-to-all-start.2) | async-done | bytes 393248 | tf_op jit(solution)/shard_map/all_to_all | solution.py:231
  60.9 1.0 %prototypes.1 = f32[86,768]{1,0:T(8,128)} custom-call(f32[8,96,128]{2,1,0:T(8,128)S(1)} %all-to-all-done.2.got_ref, f32[1,128]{1,0:T(1,128)S(1)} %get-tuple-element.19.ids_ref), custom_call_target="tpu_custom_call" | custom-call | tf_op jit(solution)/shard_map/prototypes/pallas_call | solution.py:292
Async XLA Ops:
  26.6 14.9 %all-to-all-start.1 = ((f32[8,96,128]{2,1,0:T(8,128)}), f32[8,96,128]{2,1,0:T(8,128)S(1)}, u32[]{:S(2)}, u32[]{:S(2)}) async-start(f32[8,96,128]{2,1,0:T(8,128)} %get-tuple-element.14), calls=%async_computation.1 | async-start | bytes 786432 | tf_op jit(solution)/shard_map/all_to_all | solution.py:231
  30.1 2.3 %copy-start = (bf16[3072,768]{1,0:T(8,128)(2,1)S(1)}, bf16[3072,768]{1,0:T(8,128)(2,1)}, u32[]{:S(2)}) copy-start(bf16[3072,768]{1,0:T(8,128)(2,1)} %rows_hbm.3) | copy-start | bytes 14155780
  45.7 15.2 %all-to-all-start.2 = ((f32[8,96,128]{2,1,0:T(8,128)}), f32[8,96,128]{2,1,0:T(8,128)S(1)}, u32[]{:S(2)}, u32[]{:S(2)}) async-start(f32[8,96,128]{2,1,0:T(8,128)} %get-tuple-element.18), calls=%async_computation.2 | async-start | bytes 786432 | tf_op jit(solution)/shard_map/all_to_all | solution.py:231
  49.4 1.9 %collective-permute-start.2 = (f32[3072]{0:T(1024)S(1)}, f32[3072]{0:T(1024)S(1)}, u32[]{:S(2)}, u32[]{:S(2)}) collective-permute-start(f32[3072]{0:T(1024)S(1)} %bitcast.4), channel_id=1, source_target_pairs={{0,3},{1,0},{2,1},{3,2},{4,7},{5,4},{6,5},{7,6},{8,11},{9,8},{10,9... | collective-permute-start | bytes 36872 | tf_op jit(solution)/shard_map/ppermute | solution.py:291
  49.8 3.7 %collective-permute-start.1 = (f32[3072]{0:T(1024)S(1)}, f32[3072]{0:T(1024)S(1)}, u32[]{:S(2)}, u32[]{:S(2)}) collective-permute-start(f32[3072]{0:T(1024)S(1)} %bitcast.5), channel_id=1, source_target_pairs={{0,2},{1,3},{2,0},{3,1},{4,6},{5,7},{6,4},{7,5},{8,10},{9,11},{10,... | collective-permute-start | bytes 36872 | tf_op jit(solution)/shard_map/ppermute | solution.py:291
  51.0 3.1 %collective-permute-start = (f32[3072]{0:T(1024)S(1)}, f32[3072]{0:T(1024)S(1)}, u32[]{:S(2)}, u32[]{:S(2)}) collective-permute-start(f32[3072]{0:T(1024)S(1)} %bitcast.6), channel_id=1, source_target_pairs={{0,1},{1,2},{2,3},{3,0},{4,5},{5,6},{6,7},{7,4},{8,9},{9,10},{10,1... | collective-permute-start | bytes 36872 | tf_op jit(solution)/shard_map/ppermute | solution.py:291

commit v4 on v3

--- a/solution.py
+++ b/solution.py
@@ -69,6 +69,10 @@
     return [0, first, row_total] if first else [0, row_total]
 
 
+def is_early(my_group):
+    return my_group % 2 == 0
+
+
 def fetch_rows(rows_hbm, rows_ref, row_sems, cuts):
     copies = []
     for t in range(len(cuts) - 1):
@@ -78,7 +82,7 @@
     return copies
 
 
-def sums_kernel(group_count, place_ref, label_hbm, rows_hbm, out_ref, slot_ref, label_ref, rows_ref, label_sem, row_sems):
+def sums_kernel(group_count, place_ref, label_hbm, rows_hbm, out_ref, slot_ref, length_ref, label_ref, rows_ref, label_sem, row_sems):
     owner_count = out_ref.shape[0]
     slot_total = owner_count * SLOTS
     row_total, width = rows_ref.shape
@@ -87,7 +91,7 @@
     label_copy = pltpu.make_async_copy(label_hbm, label_ref, label_sem)
     label_copy.start()
     row_copies = fetch_rows(rows_hbm, rows_ref, row_sems, cuts)
-    my_group, my_owner, live = place_ref[0], place_ref[1], place_ref[2]
+    my_group, my_place, live = place_ref[0], place_ref[1], place_ref[2]
     label_copy.wait()
     label = label_ref[...].astype(jnp.float32)
     block = jnp.floor((label + 0.5) * (1.0 / CLS_DEV))
@@ -98,7 +102,8 @@
     owned = (group == my_group.astype(jnp.float32)) & (position < live)
     owner = jnp.where(owned, owner, -1.0)
     owner_pad = max(owner_count, 16)
-    by_owner = iota((owner_pad, row_total), 0) == owner
+    places = lax.broadcasted_iota(jnp.int32, (owner_pad, 1), 0)
+    by_owner = owner_at(places, owner_count).astype(jnp.float32) == owner
     by_class = flags(iota((LANES, row_total), 0) == inner)
     counts = dot(flags(by_owner), by_class, ((1,), (1,)))
     present = counts > 0
@@ -106,11 +111,12 @@
     rank = dot(flags(present), upto, ((1,), (0,))) - 1.0
     slot = jnp.where(present, rank, -1.0)
     row_slots = dot(slot.astype(jnp.bfloat16), by_class, ((1,), (0,)))
+    row_slots = row_slots + (places * SLOTS).astype(jnp.float32)
     row_slot = jnp.sum(jnp.where(by_owner, row_slots, 0.0), axis=0, keepdims=True)
-    where_to = jnp.where(owned, owner * SLOTS + row_slot, -1.0)
+    where_to = jnp.where(owned, row_slot, -1.0)
     slot_ref[...] = where_to
     class_at = iota((owner_pad, LANES), 1)
-    lane = lax.broadcasted_iota(jnp.int32, (owner_pad, slot_total), 1) - my_owner * SLOTS
+    lane = lax.broadcasted_iota(jnp.int32, (owner_pad, slot_total), 1) - my_place * SLOTS
     ids = jnp.zeros((owner_pad, slot_total), jnp.float32)
     tally = jnp.zeros((owner_pad, slot_total), jnp.float32)
     for s in range(SLOTS):
@@ -135,6 +141,14 @@
         total = product if total is None else total + product
     put_slots(out_ref, total)
 
+    @pl.when(is_early(my_group))
+    def work():
+        measure_rows(rows_ref, length_ref)
+
+    @pl.when(jnp.logical_not(is_early(my_group)))
+    def later():
+        length_ref[...] = jnp.zeros_like(length_ref)
+
 
 def means_kernel(got_ref, means_ref, back_ref, ids_ref):
     owner_count = got_ref.shape[0]
@@ -161,16 +175,27 @@
     put_slots(back_ref, pick(onehot, unit, 0))
 
 
-def lengths_kernel(rows_ref, out_ref, head_ref):
+def measure_rows(rows_ref, out_ref):
     row_total, width = rows_ref.shape
     tile = min(512, row_total)
     ones = jnp.ones((16, width), jnp.bfloat16)
-    head_ref[...] = rows_ref[:head_ref.shape[0], :]
     for t in range(row_total // tile):
         features = rows_ref[t * tile:(t + 1) * tile, :].astype(jnp.float32)
         hi, lo = split2(features * features)
         total = dot(ones, hi, ((1,), (1,))) + dot(ones, lo, ((1,), (1,)))
         out_ref[:, t * tile:(t + 1) * tile] = jnp.sqrt(total[0:1] + epsilon)
+
+
+def lengths_kernel(place_ref, rows_ref, early_ref, out_ref, head_ref):
+    head_ref[...] = rows_ref[:head_ref.shape[0], :]
+
+    @pl.when(is_early(place_ref[0]))
+    def take():
+        out_ref[...] = early_ref[...]
+
+    @pl.when(jnp.logical_not(is_early(place_ref[0])))
+    def work():
+        measure_rows(rows_ref, out_ref)
 
 
 def weigh_kernel(unit_ref, head_ref, rows_hbm, slot_ref, length_ref, out_ref, sim_ref, weight_ref, tail_ref, tail_sem):
@@ -227,8 +252,33 @@
     return pltpu.with_memory_space_constraint(array, pltpu.MemorySpace.HBM)
 
 
+def owner_order(owner_count):
+    quarter = owner_count // 4
+    if owner_count % 4:
+        return list(range(owner_count))
+    return [*range(2 * quarter, 3 * quarter), *range(2 * quarter), *range(3 * quarter, owner_count)]
+
+
+def owner_at(place, owner_count):
+    order = owner_order(owner_count)
+    owner = place
+    for position in range(owner_count):
+        if order[position] != position:
+            owner = jnp.where(place == position, order[position], owner)
+    return owner
+
+
+def place_of(owner, owner_count):
+    place = owner
+    for position, known in enumerate(owner_order(owner_count)):
+        if known != position:
+            place = jnp.where(owner == known, position, place)
+    return place
+
+
 def exchange(payload):
-    return lax.all_to_all(payload, "dp", split_axis=0, concat_axis=0, tiled=True)
+    order = owner_order(payload.shape[0])
+    return lax.all_to_all(payload, "dp", split_axis=0, concat_axis=0, tiled=True, axis_index_groups=[order])
 
 
 def shards(embeddings, labels, row_count):
@@ -239,12 +289,14 @@
     pieces = width // LANES
     slot_rows = pieces * SLOTS
     meta_rows = 8 * (slot_total // LANES)
-    place = jnp.stack([lax.axis_index("cls"), lax.axis_index("dp"), row_count[0]]).astype(jnp.int32)
-    payload, where_to = call(
+    my_place = place_of(lax.axis_index("dp"), owner_count)
+    place = jnp.stack([lax.axis_index("cls"), my_place, row_count[0]]).astype(jnp.int32)
+    payload, where_to, early_lengths = call(
         functools.partial(sums_kernel, group_count),
         [SMEM, HBM, HBM],
         [
             (owner_count, slot_rows + meta_rows, LANES),
+            (1, row_total),
             (1, row_total),
         ],
         "sums",
@@ -260,11 +312,11 @@
     head = row_total // 2
     lengths, head_rows = call(
         lengths_kernel,
-        [VMEM],
+        [SMEM, VMEM, VMEM],
         [(1, row_total), jax.ShapeDtypeStruct((head, width), jnp.bfloat16)],
         "lengths",
         cost=cost,
-    )(embeddings)
+    )(place, embeddings, early_lengths)
     class_means, back, ids = call(
         means_kernel,
         [VMEM],

time: 62.3 us -> 53.4 us (0.86)
  waiting for transfers between devices: 15.4 us -> 7.41 us
  blocking collectives: 19.7 us -> 15.7 us
  starting transfers between devices: 8.86 us -> 11.3 us
    all_to_all x2, waiting for transfers between devices: 12.5 us -> 4.52 us  [exchange(): lax.all_to_all(payload, 'dp', split_axis=0, concat_axis=0, tiled=True, ax...]
    all_to_all x1, blocking collectives: 19.7 us -> 15.7 us  [exchange(): lax.all_to_all(payload, 'dp', split_axis=0, concat_axis=0, tiled=True, ax...]
    pallas_call x1, Pallas kernels: 4.31 us -> 6.98 us  [shards(): call(functools.partial(sums_kernel, group_count), [SMEM, HBM, HBM], [(own...]
    all_to_all x2, starting transfers between devices: 7.11 us -> 9.59 us  [exchange(): lax.all_to_all(payload, 'dp', split_axis=0, concat_axis=0, tiled=True, ax...]
    pallas_call x1, Pallas kernels: 2.8 us -> 0.7 us  [shards(): call(lengths_kernel, [SMEM, VMEM, VMEM], [(1, row_total), jax.ShapeDtypeS...]
  transfers between devices with their start and end apart: 5 -> 5, of which waited for: 5 -> 4; matrix products, arithmetic and copies ran while one was open for 1% -> 1% of each run, Pallas kernels for 5% -> 1%
where the time goes in v4:
time: 53.4 us; the launch traced here: 53 us
  blocking collectives  15.7 us (29%)
  Pallas kernels  14.1 us (26%)
  starting transfers between devices  11.3 us (21%)
  waiting for transfers between devices  7.41 us (14%)
  local copies, waits for them, and re-layouts  2.34 us (4%)
  between operations  1.33 us (2%)
  other arithmetic  0.68 us (1%)
    all_to_all x1, blocking collectives, exchange(): lax.all_to_all(payload, 'dp', split_axis=0, concat_axis=0, tiled=True, ax...  15.7 us
    all_to_all x2, starting transfers between devices, exchange(): lax.all_to_all(payload, 'dp', split_axis=0, concat_axis=0, tiled=True, ax...  9.59 us
    pallas_call x1, Pallas kernels, shards(): call(functools.partial(sums_kernel, group_count), [SMEM, HBM, HBM], [(own...  6.98 us
    all_to_all x2, waiting for transfers between devices, exchange(): lax.all_to_all(payload, 'dp', split_axis=0, concat_axis=0, tiled=True, ax...  4.52 us
    pallas_call x1, Pallas kernels, shards(): call(weigh_kernel, [VMEM, VMEM, HBM, VMEM, VMEM], [(owner_count, slot_row...  4.18 us
    ppermute x3, waiting for transfers between devices, shards(): similarity = similarity + lax.ppermute(own, 'cls', ring)  2.89 us
    unnamed x2, local copies, waits for them, and re-layouts  2.34 us
    ppermute x3, starting transfers between devices, shards(): similarity = similarity + lax.ppermute(own, 'cls', ring)  1.75 us
  transfers between devices with their start and end apart: 5, of which 4 were waited for; matrix products, arithmetic and copies ran while one was open for 1% of the time, Pallas kernels for 1%

profile of v4, /device:TPU:0, one launch (start us, length us, event | category | flops | bytes accessed | tf_op | source)
XLA Modules:
  0.0 53.0 jit_solution(513924234490119330)
XLA Ops:
  1.3 0.1 pad_add_fusion.place_ref
  1.4 7.0 %sums.1 = (f32[8,104,128]{2,1,0:T(8,128)S(1)}, f32[1,3072]{1,0:T(1,128)S(1)}, f32[1,3072]{1,0:T(1,128)S(1)}) custom-call(s32[3]{0:T(128)S(1)} %pad_add_fusion.place_ref, s32[1,3072]{1,0:T(1,128)} %bitcast.8, bf16[3072,768]{1,0:T(8,128)(2,1)} %rows_hbm.3), custom_call_target="tpu_custom_call" | custom-call | tf_op jit(solution)/shard_map/sums/pallas_call | solution.py:294
  8.4 15.7 %all_to_all.15.got_ref = f32[8,104,128]{2,1,0:T(8,128)S(1)} all-to-all(f32[8,104,128]{2,1,0:T(8,128)S(1)} %get-tuple-element.13), channel_id=1, replica_groups={{16,20,0,4,8,12,24,28},{17,21,1,5,9,13,25,29},{18,22,2,6,10,14,26,30},{..., dimensions={0} | all-to-all | bytes 851968 | tf_op jit(solution)/shard_map/all_to_all | solution.py:281
  24.1 1.3 %means.1 = (f32[86,768]{1,0:T(8,128)}, f32[8,96,128]{2,1,0:T(8,128)}, f32[1,128]{1,0:T(1,128)S(1)}) custom-call(f32[8,104,128]{2,1,0:T(8,128)S(1)} %all_to_all.15.got_ref), custom_call_target="tpu_custom_call" | custom-call | tf_op jit(solution)/shard_map/means/pallas_call | solution.py:320
  25.4 4.3 %all-to-all-start.1 = ((f32[8,96,128]{2,1,0:T(8,128)}), f32[8,96,128]{2,1,0:T(8,128)S(1)}, u32[]{:S(2)}, u32[]{:S(2)}) async-start(f32[8,96,128]{2,1,0:T(8,128)} %get-tuple-element.15), calls=%async_computation.1 | async-start | bytes 786432 | tf_op jit(solution)/shard_map/all_to_all | solution.py:281
  29.7 0.0 copy-start
  29.7 2.3 %copy-done = bf16[3072,768]{1,0:T(8,128)(2,1)S(1)} copy-done((bf16[3072,768]{1,0:T(8,128)(2,1)S(1)}, bf16[3072,768]{1,0:T(8,128)(2,1)}, u32[]{:S(2)}) %copy-start) | copy-done | bytes 4718616
  32.0 0.7 %lengths.1 = (f32[1,3072]{1,0:T(1,128)S(1)}, bf16[1536,768]{1,0:T(8,128)(2,1)S(1)}) custom-call(s32[3]{0:T(128)S(1)} %pad_add_fusion.place_ref, bf16[3072,768]{1,0:T(8,128)(2,1)S(1)} %copy-done, f32[1,3072]{1,0:T(1,128)S(1)} %get-tuple-element.16.early_ref), custom_call_target="tpu_custom_call" | custom-call | flops 2415919104 | bytes 4718592 | tf_op jit(solution)/shard_map/lengths/pallas_call | solution.py:313
  32.8 3.4 %all-to-all-done.1.unit_ref = f32[8,96,128]{2,1,0:T(8,128)S(1)} async-done(((f32[8,96,128]{2,1,0:T(8,128)}), f32[8,96,128]{2,1,0:T(8,128)S(1)}, u32[]{:S(2)}, u32[]{:S(2)}) %all-to-all-start.1) | async-done | bytes 393248 | tf_op jit(solution)/shard_map/all_to_all | solution.py:281
  36.1 4.2 %weigh.1 = (f32[8,96,128]{2,1,0:T(8,128)}, f32[1,3072]{1,0:T(1,128)S(1)}) custom-call(f32[8,96,128]{2,1,0:T(8,128)S(1)} %all-to-all-done.1.unit_ref, bf16[1536,768]{1,0:T(8,128)(2,1)S(1)} %get-tuple-element.17.head_ref, bf16[3072,768]{1,0:T(8,128)(2,1)} %rows_hbm.3, f32[1,3072]{1,0:T(1,128)S(1)} %get-tuple-element.18.slot_ref, ...), custom_call_target="tpu_custom_call" | custom-call | tf_op jit(solution)/shard_map/weigh/pallas_call | solution.py:327
  40.3 5.3 %all-to-all-start.2 = ((f32[8,96,128]{2,1,0:T(8,128)}), f32[8,96,128]{2,1,0:T(8,128)S(1)}, u32[]{:S(2)}, u32[]{:S(2)}) async-start(f32[8,96,128]{2,1,0:T(8,128)} %get-tuple-element.20), calls=%async_computation.2 | async-start | bytes 786432 | tf_op jit(solution)/shard_map/all_to_all | solution.py:281
  45.5 0.0 collective-permute-start.2
  45.5 1.5 %collective-permute-start.1 = (f32[3072]{0:T(1024)S(1)}, f32[3072]{0:T(1024)S(1)}, u32[]{:S(2)}, u32[]{:S(2)}) collective-permute-start(f32[3072]{0:T(1024)S(1)} %bitcast.5), channel_id=1, source_target_pairs={{0,2},{1,3},{2,0},{3,1},{4,6},{5,7},{6,4},{7,5},{8,10},{9,11},{10,... | collective-permute-start | bytes 36872 | tf_op jit(solution)/shard_map/ppermute | solution.py:343
  47.1 0.2 collective-permute-start
  47.3 0.0 collective-permute-done.2
  47.3 1.9 %collective-permute-done.1 = f32[3072]{0:T(1024)S(1)} collective-permute-done((f32[3072]{0:T(1024)S(1)}, f32[3072]{0:T(1024)S(1)}, u32[]{:S(2)}, u32[]{:S(2)}) %collective-permute-start.1) | collective-permute-done | bytes 12320 | tf_op jit(solution)/shard_map/ppermute | solution.py:343
  49.2 0.9 %collective-permute-done = f32[3072]{0:T(1024)S(1)} collective-permute-done((f32[3072]{0:T(1024)S(1)}, f32[3072]{0:T(1024)S(1)}, u32[]{:S(2)}, u32[]{:S(2)}) %collective-permute-start) | collective-permute-done | bytes 12320 | tf_op jit(solution)/shard_map/ppermute | solution.py:343
  50.2 0.6 %add_add_fusion = f32[3072]{0:T(1024)} fusion(f32[3072]{0:T(1024)S(1)} %collective-permute-done.2, f32[3072]{0:T(1024)S(1)} %collective-permute-done.1, f32[3072]{0:T(1024)S(1)} %bitcast.7, f32[3072]{0:T(1024)S(1)} %collective-permute-done), kind=kLoop, calls=%fused_computation | loop fusion | flops 9216 | bytes 61440 | tf_op jit(solution)/shard_map/add | solution.py:343
  50.8 1.2 %all-to-all-done.2.got_ref = f32[8,96,128]{2,1,0:T(8,128)S(1)} async-done(((f32[8,96,128]{2,1,0:T(8,128)}), f32[8,96,128]{2,1,0:T(8,128)S(1)}, u32[]{:S(2)}, u32[]{:S(2)}) %all-to-all-start.2) | async-done | bytes 393248 | tf_op jit(solution)/shard_map/all_to_all | solution.py:281
  52.0 1.0 %prototypes.1 = f32[86,768]{1,0:T(8,128)} custom-call(f32[8,96,128]{2,1,0:T(8,128)S(1)} %all-to-all-done.2.got_ref, f32[1,128]{1,0:T(1,128)S(1)} %get-tuple-element.21.ids_ref), custom_call_target="tpu_custom_call" | custom-call | tf_op jit(solution)/shard_map/prototypes/pallas_call | solution.py:344
Async XLA Ops:
  25.4 10.7 %all-to-all-start.1 = ((f32[8,96,128]{2,1,0:T(8,128)}), f32[8,96,128]{2,1,0:T(8,128)S(1)}, u32[]{:S(2)}, u32[]{:S(2)}) async-start(f32[8,96,128]{2,1,0:T(8,128)} %get-tuple-element.15), calls=%async_computation.1 | async-start | bytes 786432 | tf_op jit(solution)/shard_map/all_to_all | solution.py:281
  29.7 2.3 %copy-start = (bf16[3072,768]{1,0:T(8,128)(2,1)S(1)}, bf16[3072,768]{1,0:T(8,128)(2,1)}, u32[]{:S(2)}) copy-start(bf16[3072,768]{1,0:T(8,128)(2,1)} %rows_hbm.3) | copy-start | bytes 14155780
  40.3 11.7 %all-to-all-start.2 = ((f32[8,96,128]{2,1,0:T(8,128)}), f32[8,96,128]{2,1,0:T(8,128)S(1)}, u32[]{:S(2)}, u32[]{:S(2)}) async-start(f32[8,96,128]{2,1,0:T(8,128)} %get-tuple-element.20), calls=%async_computation.2 | async-start | bytes 786432 | tf_op jit(solution)/shard_map/all_to_all | solution.py:281
  45.5 1.8 %collective-permute-start.2 = (f32[3072]{0:T(1024)S(1)}, f32[3072]{0:T(1024)S(1)}, u32[]{:S(2)}, u32[]{:S(2)}) collective-permute-start(f32[3072]{0:T(1024)S(1)} %bitcast.4), channel_id=1, source_target_pairs={{0,3},{1,0},{2,1},{3,2},{4,7},{5,4},{6,5},{7,6},{8,11},{9,8},{10,9... | collective-permute-start | bytes 36872 | tf_op jit(solution)/shard_map/ppermute | solution.py:343
  45.5 3.7 %collective-permute-start.1 = (f32[3072]{0:T(1024)S(1)}, f32[3072]{0:T(1024)S(1)}, u32[]{:S(2)}, u32[]{:S(2)}) collective-permute-start(f32[3072]{0:T(1024)S(1)} %bitcast.5), channel_id=1, source_target_pairs={{0,2},{1,3},{2,0},{3,1},{4,6},{5,7},{6,4},{7,5},{8,10},{9,11},{10,... | collective-permute-start | bytes 36872 | tf_op jit(solution)/shard_map/ppermute | solution.py:343
  47.1 3.1 %collective-permute-start = (f32[3072]{0:T(1024)S(1)}, f32[3072]{0:T(1024)S(1)}, u32[]{:S(2)}, u32[]{:S(2)}) collective-permute-start(f32[3072]{0:T(1024)S(1)} %bitcast.6), channel_id=1, source_target_pairs={{0,1},{1,2},{2,3},{3,0},{4,5},{5,6},{6,7},{7,4},{8,9},{9,10},{10,1... | collective-permute-start | bytes 36872 | tf_op jit(solution)/shard_map/ppermute | solution.py:343

commit v5 on v4

--- a/solution.py
+++ b/solution.py
@@ -16,7 +16,6 @@
 sharpness = 4.0
 
 VMEM = pl.BlockSpec(memory_space=pltpu.VMEM)
-SMEM = pl.BlockSpec(memory_space=pltpu.SMEM)
 HBM = pl.BlockSpec(memory_space=pltpu.MemorySpace.HBM)
 VMEM_LIMIT = 24 * 1024 * 1024
 
@@ -82,7 +81,7 @@
     return copies
 
 
-def sums_kernel(group_count, place_ref, label_hbm, rows_hbm, out_ref, slot_ref, length_ref, label_ref, rows_ref, label_sem, row_sems):
+def sums_kernel(group_count, live_ref, label_hbm, rows_hbm, out_ref, slot_ref, length_ref, label_ref, rows_ref, label_sem, row_sems):
     owner_count = out_ref.shape[0]
     slot_total = owner_count * SLOTS
     row_total, width = rows_ref.shape
@@ -91,7 +90,9 @@
     label_copy = pltpu.make_async_copy(label_hbm, label_ref, label_sem)
     label_copy.start()
     row_copies = fetch_rows(rows_hbm, rows_ref, row_sems, cuts)
-    my_group, my_place, live = place_ref[0], place_ref[1], place_ref[2]
+    my_group = lax.axis_index("cls")
+    my_place = place_of(lax.axis_index("dp"), owner_count)
+    live = live_ref[0]
     label_copy.wait()
     label = label_ref[...].astype(jnp.float32)
     block = jnp.floor((label + 0.5) * (1.0 / CLS_DEV))
@@ -115,6 +116,13 @@
     row_slot = jnp.sum(jnp.where(by_owner, row_slots, 0.0), axis=0, keepdims=True)
     where_to = jnp.where(owned, row_slot, -1.0)
     slot_ref[...] = where_to
+    total = None
+    for t in range(len(cuts) - 1):
+        part = slice(cuts[t], cuts[t + 1])
+        onehot = flags(iota((slot_total, cuts[t + 1] - cuts[t]), 0) == where_to[:, part])
+        row_copies[t].wait()
+        product = dot(onehot, rows_ref[part, :], ((1,), (0,)))
+        total = product if total is None else total + product
     class_at = iota((owner_pad, LANES), 1)
     lane = lax.broadcasted_iota(jnp.int32, (owner_pad, slot_total), 1) - my_place * SLOTS
     ids = jnp.zeros((owner_pad, slot_total), jnp.float32)
@@ -132,13 +140,6 @@
             meta = jnp.where(sub == 0, ids[o:o + 1, lanes], jnp.where(sub == 1, tally[o:o + 1, lanes], 0.0))
             base = pieces * SLOTS + 8 * t
             out_ref[o, base:base + 8, :] = meta
-    total = None
-    for t in range(len(cuts) - 1):
-        part = slice(cuts[t], cuts[t + 1])
-        onehot = flags(iota((slot_total, cuts[t + 1] - cuts[t]), 0) == where_to[:, part])
-        row_copies[t].wait()
-        product = dot(onehot, rows_ref[part, :], ((1,), (0,)))
-        total = product if total is None else total + product
     put_slots(out_ref, total)
 
     @pl.when(is_early(my_group))
@@ -186,14 +187,15 @@
         out_ref[:, t * tile:(t + 1) * tile] = jnp.sqrt(total[0:1] + epsilon)
 
 
-def lengths_kernel(place_ref, rows_ref, early_ref, out_ref, head_ref):
+def lengths_kernel(rows_ref, early_ref, out_ref, head_ref):
+    my_group = lax.axis_index("cls")
     head_ref[...] = rows_ref[:head_ref.shape[0], :]
 
-    @pl.when(is_early(place_ref[0]))
+    @pl.when(is_early(my_group))
     def take():
         out_ref[...] = early_ref[...]
 
-    @pl.when(jnp.logical_not(is_early(place_ref[0])))
+    @pl.when(jnp.logical_not(is_early(my_group)))
     def work():
         measure_rows(rows_ref, out_ref)
 
@@ -204,13 +206,10 @@
     tail_copy = pltpu.make_async_copy(rows_hbm.at[pl.ds(head_total, tail_ref.shape[0])], tail_ref, tail_sem)
     tail_copy.start()
     units = jnp.concatenate(split2(get_slots(unit_ref, width // LANES)), axis=0)
-    total = None
-    for rows_ref, first in ((head_ref, 0), (tail_ref, head_total)):
-        part = slice(first, first + rows_ref.shape[0])
+
+    def weights_of(rows_ref, part):
         where_to = slot_ref[:, part]
         hit = iota((slot_total, rows_ref.shape[0]), 0) == where_to
-        if first:
-            tail_copy.wait()
         products = dot(units, rows_ref[...], ((1,), (1,)))
         product = jnp.sum(
             jnp.where(hit, products[:slot_total] + products[slot_total:], 0.0), axis=0, keepdims=True
@@ -219,9 +218,13 @@
         sim_ref[:, part] = similarity
         weight = jnp.exp(sharpness * (similarity - 1.0))
         weight_ref[:, part] = jnp.where(hit, weight, 0.0).astype(jnp.bfloat16)
-        weighted = dot(weight_ref[:, part], rows_ref[...], ((1,), (0,)))
-        total = weighted if total is None else total + weighted
-    put_slots(out_ref, total)
+
+    front, back = slice(0, head_total), slice(head_total, head_total + tail_ref.shape[0])
+    weights_of(head_ref, front)
+    tail_copy.wait()
+    total = dot(weight_ref[:, front], head_ref[...], ((1,), (0,)))
+    weights_of(tail_ref, back)
+    put_slots(out_ref, total + dot(weight_ref[:, back], tail_ref[...], ((1,), (0,))))
 
 
 def prototypes_kernel(got_ref, ids_ref, out_ref):
@@ -289,11 +292,9 @@
     pieces = width // LANES
     slot_rows = pieces * SLOTS
     meta_rows = 8 * (slot_total // LANES)
-    my_place = place_of(lax.axis_index("dp"), owner_count)
-    place = jnp.stack([lax.axis_index("cls"), my_place, row_count[0]]).astype(jnp.int32)
     payload, where_to, early_lengths = call(
         functools.partial(sums_kernel, group_count),
-        [SMEM, HBM, HBM],
+        [pl.BlockSpec(memory_space=pltpu.SMEM), HBM, HBM],
         [
             (owner_count, slot_rows + meta_rows, LANES),
             (1, row_total),
@@ -306,17 +307,17 @@
             pltpu.SemaphoreType.DMA,
             pltpu.SemaphoreType.DMA((len(row_cuts(row_total)) - 1,)),
         ],
-    )(place, in_hbm(labels.reshape(1, row_total)), in_hbm(embeddings))
+    )(row_count, in_hbm(labels.reshape(1, row_total)), in_hbm(embeddings))
     got = exchange(payload)
     cost = pl.CostEstimate(flops=8 * row_total * width * 128, bytes_accessed=2 * row_total * width, transcendentals=row_total)
-    head = row_total // 2
+    head = row_total * 7 // 12 // 256 * 256
     lengths, head_rows = call(
         lengths_kernel,
-        [SMEM, VMEM, VMEM],
+        [VMEM, VMEM],
         [(1, row_total), jax.ShapeDtypeStruct((head, width), jnp.bfloat16)],
         "lengths",
         cost=cost,
-    )(place, embeddings, early_lengths)
+    )(embeddings, early_lengths)
     class_means, back, ids = call(
         means_kernel,
         [VMEM],

time: 53.4 us -> 52.7 us (0.987)
  Pallas kernels: 14.1 us -> 13 us
    pallas_call x2, Pallas kernels: 7.68 us -> 6.62 us  [the longest x1 6.44 us: shards(): call(functools.partial(sums_kernel, group_count), [pl.BlockSpec(memory_sp...]
  transfers between devices with their start and end apart: 5 -> 5, of which waited for: 4 -> 4; matrix products, arithmetic and copies ran while one was open for 1% -> 1% of each run, Pallas kernels for 1% -> 0%
where the time goes in v5:
time: 52.7 us; the launch traced here: 52.3 us
  blocking collectives  15.7 us (30%)
  Pallas kernels  13 us (25%)
  starting transfers between devices  11.3 us (21%)
  waiting for transfers between devices  7.94 us (15%)
  local copies, waits for them, and re-layouts  2.34 us (4%)
  between operations  1.31 us (2%)
  other arithmetic  0.6 us (1%)
    all_to_all x1, blocking collectives, exchange(): lax.all_to_all(payload, 'dp', split_axis=0, concat_axis=0, tiled=True, ax...  15.7 us
    all_to_all x2, starting transfers between devices, exchange(): lax.all_to_all(payload, 'dp', split_axis=0, concat_axis=0, tiled=True, ax...  9.59 us
    pallas_call x1, Pallas kernels, shards(): call(functools.partial(sums_kernel, group_count), [pl.BlockSpec(memory_sp...  6.44 us
    all_to_all x2, waiting for transfers between devices, exchange(): lax.all_to_all(payload, 'dp', split_axis=0, concat_axis=0, tiled=True, ax...  5.04 us
    pallas_call x1, Pallas kernels, shards(): call(weigh_kernel, [VMEM, VMEM, HBM, VMEM, VMEM], [(owner_count, slot_row...  4.13 us
    ppermute x3, waiting for transfers between devices, shards(): similarity = similarity + lax.ppermute(own, 'cls', ring)  2.89 us
    unnamed x2, local copies, waits for them, and re-layouts  2.34 us
    ppermute x3, starting transfers between devices, shards(): similarity = similarity + lax.ppermute(own, 'cls', ring)  1.75 us
  transfers between devices with their start and end apart: 5, of which 4 were waited for; matrix products, arithmetic and copies ran while one was open for 1% of the time, Pallas kernels for 0%

profile of v5, /device:TPU:0, one launch (start us, length us, event | category | flops | bytes accessed | tf_op | source)
XLA Modules:
  0.0 52.3 jit_solution(6723983616442675901)
XLA Ops:
  1.3 6.4 %sums.1 = (f32[8,104,128]{2,1,0:T(8,128)S(1)}, f32[1,3072]{1,0:T(1,128)S(1)}, f32[1,3072]{1,0:T(1,128)S(1)}) custom-call(s32[1]{0:T(128)S(6)} %copy.6.live_ref, s32[1,3072]{1,0:T(1,128)} %bitcast.6, bf16[3072,768]{1,0:T(8,128)(2,1)} %rows_hbm.3), custom_call_target="tpu_custom_call" | custom-call | tf_op jit(solution)/shard_map/sums/pallas_call | solution.py:295
  7.7 15.7 %all_to_all.15.got_ref = f32[8,104,128]{2,1,0:T(8,128)S(1)} all-to-all(f32[8,104,128]{2,1,0:T(8,128)S(1)} %get-tuple-element.13), channel_id=1, replica_groups={{16,20,0,4,8,12,24,28},{17,21,1,5,9,13,25,29},{18,22,2,6,10,14,26,30},{..., dimensions={0} | all-to-all | bytes 851968 | tf_op jit(solution)/shard_map/all_to_all | solution.py:284
  23.4 1.3 %means.1 = (f32[86,768]{1,0:T(8,128)}, f32[8,96,128]{2,1,0:T(8,128)}, f32[1,128]{1,0:T(1,128)S(1)}) custom-call(f32[8,104,128]{2,1,0:T(8,128)S(1)} %all_to_all.15.got_ref), custom_call_target="tpu_custom_call" | custom-call | tf_op jit(solution)/shard_map/means/pallas_call | solution.py:321
  24.7 4.3 %all-to-all-start.1 = ((f32[8,96,128]{2,1,0:T(8,128)}), f32[8,96,128]{2,1,0:T(8,128)S(1)}, u32[]{:S(2)}, u32[]{:S(2)}) async-start(f32[8,96,128]{2,1,0:T(8,128)} %get-tuple-element.15), calls=%async_computation.1 | async-start | bytes 786432 | tf_op jit(solution)/shard_map/all_to_all | solution.py:284
  29.1 0.0 copy-start
  29.1 2.3 %copy-done = bf16[3072,768]{1,0:T(8,128)(2,1)S(1)} copy-done((bf16[3072,768]{1,0:T(8,128)(2,1)S(1)}, bf16[3072,768]{1,0:T(8,128)(2,1)}, u32[]{:S(2)}) %copy-start) | copy-done | bytes 4718616
  31.4 0.2 lengths.1
  31.6 3.9 %all-to-all-done.1.unit_ref = f32[8,96,128]{2,1,0:T(8,128)S(1)} async-done(((f32[8,96,128]{2,1,0:T(8,128)}), f32[8,96,128]{2,1,0:T(8,128)S(1)}, u32[]{:S(2)}, u32[]{:S(2)}) %all-to-all-start.1) | async-done | bytes 393248 | tf_op jit(solution)/shard_map/all_to_all | solution.py:284
  35.5 4.1 %weigh.1 = (f32[8,96,128]{2,1,0:T(8,128)}, f32[1,3072]{1,0:T(1,128)S(1)}) custom-call(f32[8,96,128]{2,1,0:T(8,128)S(1)} %all-to-all-done.1.unit_ref, bf16[1792,768]{1,0:T(8,128)(2,1)S(1)} %get-tuple-element.17.head_ref, bf16[3072,768]{1,0:T(8,128)(2,1)} %rows_hbm.3, f32[1,3072]{1,0:T(1,128)S(1)} %get-tuple-element.18.slot_ref, ...), custom_call_target="tpu_custom_call" | custom-call | tf_op jit(solution)/shard_map/weigh/pallas_call | solution.py:328
  39.6 5.3 %all-to-all-start.2 = ((f32[8,96,128]{2,1,0:T(8,128)}), f32[8,96,128]{2,1,0:T(8,128)S(1)}, u32[]{:S(2)}, u32[]{:S(2)}) async-start(f32[8,96,128]{2,1,0:T(8,128)} %get-tuple-element.20), calls=%async_computation.2 | async-start | bytes 786432 | tf_op jit(solution)/shard_map/all_to_all | solution.py:284
  44.9 0.0 collective-permute-start.2
  44.9 1.5 %collective-permute-start.1 = (f32[3072]{0:T(1024)S(1)}, f32[3072]{0:T(1024)S(1)}, u32[]{:S(2)}, u32[]{:S(2)}) collective-permute-start(f32[3072]{0:T(1024)S(1)} %bitcast.3), channel_id=1, source_target_pairs={{0,2},{1,3},{2,0},{3,1},{4,6},{5,7},{6,4},{7,5},{8,10},{9,11},{10,... | collective-permute-start | bytes 36872 | tf_op jit(solution)/shard_map/ppermute | solution.py:344
  46.4 0.2 collective-permute-start
  46.6 0.0 collective-permute-done.2
  46.6 1.9 %collective-permute-done.1 = f32[3072]{0:T(1024)S(1)} collective-permute-done((f32[3072]{0:T(1024)S(1)}, f32[3072]{0:T(1024)S(1)}, u32[]{:S(2)}, u32[]{:S(2)}) %collective-permute-start.1) | collective-permute-done | bytes 12320 | tf_op jit(solution)/shard_map/ppermute | solution.py:344
  48.6 0.9 %collective-permute-done = f32[3072]{0:T(1024)S(1)} collective-permute-done((f32[3072]{0:T(1024)S(1)}, f32[3072]{0:T(1024)S(1)}, u32[]{:S(2)}, u32[]{:S(2)}) %collective-permute-start) | collective-permute-done | bytes 12320 | tf_op jit(solution)/shard_map/ppermute | solution.py:344
  49.5 0.6 %add_add_fusion = f32[3072]{0:T(1024)} fusion(f32[3072]{0:T(1024)S(1)} %collective-permute-done.2, f32[3072]{0:T(1024)S(1)} %collective-permute-done.1, f32[3072]{0:T(1024)S(1)} %bitcast.5, f32[3072]{0:T(1024)S(1)} %collective-permute-done), kind=kLoop, calls=%fused_computation | loop fusion | flops 9216 | bytes 61440 | tf_op jit(solution)/shard_map/add | solution.py:344
  50.1 1.2 %all-to-all-done.2.got_ref = f32[8,96,128]{2,1,0:T(8,128)S(1)} async-done(((f32[8,96,128]{2,1,0:T(8,128)}), f32[8,96,128]{2,1,0:T(8,128)S(1)}, u32[]{:S(2)}, u32[]{:S(2)}) %all-to-all-start.2) | async-done | bytes 393248 | tf_op jit(solution)/shard_map/all_to_all | solution.py:284
  51.3 1.0 %prototypes.1 = f32[86,768]{1,0:T(8,128)} custom-call(f32[8,96,128]{2,1,0:T(8,128)S(1)} %all-to-all-done.2.got_ref, f32[1,128]{1,0:T(1,128)S(1)} %get-tuple-element.21.ids_ref), custom_call_target="tpu_custom_call" | custom-call | tf_op jit(solution)/shard_map/prototypes/pallas_call | solution.py:345
Async XLA Ops:
  24.7 10.7 %all-to-all-start.1 = ((f32[8,96,128]{2,1,0:T(8,128)}), f32[8,96,128]{2,1,0:T(8,128)S(1)}, u32[]{:S(2)}, u32[]{:S(2)}) async-start(f32[8,96,128]{2,1,0:T(8,128)} %get-tuple-element.15), calls=%async_computation.1 | async-start | bytes 786432 | tf_op jit(solution)/shard_map/all_to_all | solution.py:284
  29.1 2.3 %copy-start = (bf16[3072,768]{1,0:T(8,128)(2,1)S(1)}, bf16[3072,768]{1,0:T(8,128)(2,1)}, u32[]{:S(2)}) copy-start(bf16[3072,768]{1,0:T(8,128)(2,1)} %rows_hbm.3) | copy-start | bytes 14155780
  39.6 11.7 %all-to-all-start.2 = ((f32[8,96,128]{2,1,0:T(8,128)}), f32[8,96,128]{2,1,0:T(8,128)S(1)}, u32[]{:S(2)}, u32[]{:S(2)}) async-start(f32[8,96,128]{2,1,0:T(8,128)} %get-tuple-element.20), calls=%async_computation.2 | async-start | bytes 786432 | tf_op jit(solution)/shard_map/all_to_all | solution.py:284
  44.9 1.8 %collective-permute-start.2 = (f32[3072]{0:T(1024)S(1)}, f32[3072]{0:T(1024)S(1)}, u32[]{:S(2)}, u32[]{:S(2)}) collective-permute-start(f32[3072]{0:T(1024)S(1)} %bitcast.2), channel_id=1, source_target_pairs={{0,3},{1,0},{2,1},{3,2},{4,7},{5,4},{6,5},{7,6},{8,11},{9,8},{10,9... | collective-permute-start | bytes 36872 | tf_op jit(solution)/shard_map/ppermute | solution.py:344
  44.9 3.7 %collective-permute-start.1 = (f32[3072]{0:T(1024)S(1)}, f32[3072]{0:T(1024)S(1)}, u32[]{:S(2)}, u32[]{:S(2)}) collective-permute-start(f32[3072]{0:T(1024)S(1)} %bitcast.3), channel_id=1, source_target_pairs={{0,2},{1,3},{2,0},{3,1},{4,6},{5,7},{6,4},{7,5},{8,10},{9,11},{10,... | collective-permute-start | bytes 36872 | tf_op jit(solution)/shard_map/ppermute | solution.py:344
  46.4 3.1 %collective-permute-start = (f32[3072]{0:T(1024)S(1)}, f32[3072]{0:T(1024)S(1)}, u32[]{:S(2)}, u32[]{:S(2)}) collective-permute-start(f32[3072]{0:T(1024)S(1)} %bitcast.4), channel_id=1, source_target_pairs={{0,1},{1,2},{2,3},{3,0},{4,5},{5,6},{6,7},{7,4},{8,9},{9,10},{10,1... | collective-permute-start | bytes 36872 | tf_op jit(solution)/shard_map/ppermute | solution.py:344

commit v6 on v5

--- a/solution.py
+++ b/solution.py
@@ -63,33 +63,19 @@
     return jnp.concatenate(rows, axis=0)
 
 
-def row_cuts(row_total):
-    first = row_total * 2 // 3 // LANES * LANES
-    return [0, first, row_total] if first else [0, row_total]
-
-
 def is_early(my_group):
     return my_group % 2 == 0
 
 
-def fetch_rows(rows_hbm, rows_ref, row_sems, cuts):
-    copies = []
-    for t in range(len(cuts) - 1):
-        part = pl.ds(cuts[t], cuts[t + 1] - cuts[t])
-        copies.append(pltpu.make_async_copy(rows_hbm.at[part], rows_ref.at[part], row_sems.at[t]))
-        copies[-1].start()
-    return copies
-
-
-def sums_kernel(group_count, live_ref, label_hbm, rows_hbm, out_ref, slot_ref, length_ref, label_ref, rows_ref, label_sem, row_sems):
+def sums_kernel(group_count, live_ref, label_hbm, rows_hbm, out_ref, slot_ref, length_ref, label_ref, rows_ref, label_sem, row_sem):
     owner_count = out_ref.shape[0]
     slot_total = owner_count * SLOTS
     row_total, width = rows_ref.shape
     pieces = width // LANES
-    cuts = row_cuts(row_total)
     label_copy = pltpu.make_async_copy(label_hbm, label_ref, label_sem)
     label_copy.start()
-    row_copies = fetch_rows(rows_hbm, rows_ref, row_sems, cuts)
+    row_copy = pltpu.make_async_copy(rows_hbm, rows_ref, row_sem)
+    row_copy.start()
     my_group = lax.axis_index("cls")
     my_place = place_of(lax.axis_index("dp"), owner_count)
     live = live_ref[0]
@@ -116,13 +102,9 @@
     row_slot = jnp.sum(jnp.where(by_owner, row_slots, 0.0), axis=0, keepdims=True)
     where_to = jnp.where(owned, row_slot, -1.0)
     slot_ref[...] = where_to
-    total = None
-    for t in range(len(cuts) - 1):
-        part = slice(cuts[t], cuts[t + 1])
-        onehot = flags(iota((slot_total, cuts[t + 1] - cuts[t]), 0) == where_to[:, part])
-        row_copies[t].wait()
-        product = dot(onehot, rows_ref[part, :], ((1,), (0,)))
-        total = product if total is None else total + product
+    onehot = flags(iota((slot_total, row_total), 0) == where_to)
+    row_copy.wait()
+    total = dot(onehot, rows_ref[...], ((1,), (0,)))
     class_at = iota((owner_pad, LANES), 1)
     lane = lax.broadcasted_iota(jnp.int32, (owner_pad, slot_total), 1) - my_place * SLOTS
     ids = jnp.zeros((owner_pad, slot_total), jnp.float32)
@@ -305,7 +287,7 @@
             pltpu.VMEM((1, row_total), jnp.int32),
             pltpu.VMEM((row_total, width), jnp.bfloat16),
             pltpu.SemaphoreType.DMA,
-            pltpu.SemaphoreType.DMA((len(row_cuts(row_total)) - 1,)),
+            pltpu.SemaphoreType.DMA,
         ],
     )(row_count, in_hbm(labels.reshape(1, row_total)), in_hbm(embeddings))
     got = exchange(payload)

time: 52.7 us -> 52.2 us (level)
  no operation moved by 1% of the time
where the time goes in v6:
time: 52.2 us; the launch traced here: 51.8 us
  blocking collectives  15.7 us (30%)
  Pallas kernels  12.5 us (24%)
  starting transfers between devices  11.3 us (22%)
  waiting for transfers between devices  7.94 us (15%)
  local copies, waits for them, and re-layouts  2.34 us (4%)
  between operations  1.31 us (3%)
  other arithmetic  0.6 us (1%)
    all_to_all x1, blocking collectives, exchange(): lax.all_to_all(payload, 'dp', split_axis=0, concat_axis=0, tiled=True, ax...  15.7 us
    all_to_all x2, starting transfers between devices, exchange(): lax.all_to_all(payload, 'dp', split_axis=0, concat_axis=0, tiled=True, ax...  9.59 us
    pallas_call x1, Pallas kernels, shards(): call(functools.partial(sums_kernel, group_count), [pl.BlockSpec(memory_sp...  5.92 us
    all_to_all x2, waiting for transfers between devices, exchange(): lax.all_to_all(payload, 'dp', split_axis=0, concat_axis=0, tiled=True, ax...  5.04 us
    pallas_call x1, Pallas kernels, shards(): call(weigh_kernel, [VMEM, VMEM, HBM, VMEM, VMEM], [(owner_count, slot_row...  4.13 us
    ppermute x3, waiting for transfers between devices, shards(): similarity = similarity + lax.ppermute(own, 'cls', ring)  2.89 us
    unnamed x2, local copies, waits for them, and re-layouts  2.34 us
    ppermute x3, starting transfers between devices, shards(): similarity = similarity + lax.ppermute(own, 'cls', ring)  1.75 us
  transfers between devices with their start and end apart: 5, of which 4 were waited for; matrix products, arithmetic and copies ran while one was open for 1% of the time, Pallas kernels for 0%

profile of v6, /device:TPU:0, one launch (start us, length us, event | category | flops | bytes accessed | tf_op | source)
XLA Modules:
  0.0 51.8 jit_solution(7104160950894615470)
XLA Ops:
  1.3 5.9 %sums.1 = (f32[8,104,128]{2,1,0:T(8,128)S(1)}, f32[1,3072]{1,0:T(1,128)S(1)}, f32[1,3072]{1,0:T(1,128)S(1)}) custom-call(s32[1]{0:T(128)S(6)} %copy.6.live_ref, s32[1,3072]{1,0:T(1,128)} %bitcast.6, bf16[3072,768]{1,0:T(8,128)(2,1)} %rows_hbm.3), custom_call_target="tpu_custom_call" | custom-call | tf_op jit(solution)/shard_map/sums/pallas_call | solution.py:277
  7.2 15.7 %all_to_all.15.got_ref = f32[8,104,128]{2,1,0:T(8,128)S(1)} all-to-all(f32[8,104,128]{2,1,0:T(8,128)S(1)} %get-tuple-element.13), channel_id=1, replica_groups={{16,20,0,4,8,12,24,28},{17,21,1,5,9,13,25,29},{18,22,2,6,10,14,26,30},{..., dimensions={0} | all-to-all | bytes 851968 | tf_op jit(solution)/shard_map/all_to_all | solution.py:266
  22.9 1.3 %means.1 = (f32[86,768]{1,0:T(8,128)}, f32[8,96,128]{2,1,0:T(8,128)}, f32[1,128]{1,0:T(1,128)S(1)}) custom-call(f32[8,104,128]{2,1,0:T(8,128)S(1)} %all_to_all.15.got_ref), custom_call_target="tpu_custom_call" | custom-call | tf_op jit(solution)/shard_map/means/pallas_call | solution.py:303
  24.2 4.3 %all-to-all-start.1 = ((f32[8,96,128]{2,1,0:T(8,128)}), f32[8,96,128]{2,1,0:T(8,128)S(1)}, u32[]{:S(2)}, u32[]{:S(2)}) async-start(f32[8,96,128]{2,1,0:T(8,128)} %get-tuple-element.15), calls=%async_computation.1 | async-start | bytes 786432 | tf_op jit(solution)/shard_map/all_to_all | solution.py:266
  28.5 0.0 copy-start
  28.5 2.3 %copy-done = bf16[3072,768]{1,0:T(8,128)(2,1)S(1)} copy-done((bf16[3072,768]{1,0:T(8,128)(2,1)S(1)}, bf16[3072,768]{1,0:T(8,128)(2,1)}, u32[]{:S(2)}) %copy-start) | copy-done | bytes 4718616
  30.9 0.2 lengths.1
  31.1 3.9 %all-to-all-done.1.unit_ref = f32[8,96,128]{2,1,0:T(8,128)S(1)} async-done(((f32[8,96,128]{2,1,0:T(8,128)}), f32[8,96,128]{2,1,0:T(8,128)S(1)}, u32[]{:S(2)}, u32[]{:S(2)}) %all-to-all-start.1) | async-done | bytes 393248 | tf_op jit(solution)/shard_map/all_to_all | solution.py:266
  34.9 4.1 %weigh.1 = (f32[8,96,128]{2,1,0:T(8,128)}, f32[1,3072]{1,0:T(1,128)S(1)}) custom-call(f32[8,96,128]{2,1,0:T(8,128)S(1)} %all-to-all-done.1.unit_ref, bf16[1792,768]{1,0:T(8,128)(2,1)S(1)} %get-tuple-element.17.head_ref, bf16[3072,768]{1,0:T(8,128)(2,1)} %rows_hbm.3, f32[1,3072]{1,0:T(1,128)S(1)} %get-tuple-element.18.slot_ref, ...), custom_call_target="tpu_custom_call" | custom-call | tf_op jit(solution)/shard_map/weigh/pallas_call | solution.py:310
  39.1 5.3 %all-to-all-start.2 = ((f32[8,96,128]{2,1,0:T(8,128)}), f32[8,96,128]{2,1,0:T(8,128)S(1)}, u32[]{:S(2)}, u32[]{:S(2)}) async-start(f32[8,96,128]{2,1,0:T(8,128)} %get-tuple-element.20), calls=%async_computation.2 | async-start | bytes 786432 | tf_op jit(solution)/shard_map/all_to_all | solution.py:266
  44.3 0.0 collective-permute-start.2
  44.3 1.5 %collective-permute-start.1 = (f32[3072]{0:T(1024)S(1)}, f32[3072]{0:T(1024)S(1)}, u32[]{:S(2)}, u32[]{:S(2)}) collective-permute-start(f32[3072]{0:T(1024)S(1)} %bitcast.3), channel_id=1, source_target_pairs={{0,2},{1,3},{2,0},{3,1},{4,6},{5,7},{6,4},{7,5},{8,10},{9,11},{10,... | collective-permute-start | bytes 36872 | tf_op jit(solution)/shard_map/ppermute | solution.py:326
  45.9 0.2 collective-permute-start
  46.1 0.0 collective-permute-done.2
  46.1 1.9 %collective-permute-done.1 = f32[3072]{0:T(1024)S(1)} collective-permute-done((f32[3072]{0:T(1024)S(1)}, f32[3072]{0:T(1024)S(1)}, u32[]{:S(2)}, u32[]{:S(2)}) %collective-permute-start.1) | collective-permute-done | bytes 12320 | tf_op jit(solution)/shard_map/ppermute | solution.py:326
  48.0 0.9 %collective-permute-done = f32[3072]{0:T(1024)S(1)} collective-permute-done((f32[3072]{0:T(1024)S(1)}, f32[3072]{0:T(1024)S(1)}, u32[]{:S(2)}, u32[]{:S(2)}) %collective-permute-start) | collective-permute-done | bytes 12320 | tf_op jit(solution)/shard_map/ppermute | solution.py:326
  49.0 0.6 %add_add_fusion = f32[3072]{0:T(1024)} fusion(f32[3072]{0:T(1024)S(1)} %collective-permute-done.2, f32[3072]{0:T(1024)S(1)} %collective-permute-done.1, f32[3072]{0:T(1024)S(1)} %bitcast.5, f32[3072]{0:T(1024)S(1)} %collective-permute-done), kind=kLoop, calls=%fused_computation | loop fusion | flops 9216 | bytes 61440 | tf_op jit(solution)/shard_map/add | solution.py:326
  49.6 1.2 %all-to-all-done.2.got_ref = f32[8,96,128]{2,1,0:T(8,128)S(1)} async-done(((f32[8,96,128]{2,1,0:T(8,128)}), f32[8,96,128]{2,1,0:T(8,128)S(1)}, u32[]{:S(2)}, u32[]{:S(2)}) %all-to-all-start.2) | async-done | bytes 393248 | tf_op jit(solution)/shard_map/all_to_all | solution.py:266
  50.7 1.0 %prototypes.1 = f32[86,768]{1,0:T(8,128)} custom-call(f32[8,96,128]{2,1,0:T(8,128)S(1)} %all-to-all-done.2.got_ref, f32[1,128]{1,0:T(1,128)S(1)} %get-tuple-element.21.ids_ref), custom_call_target="tpu_custom_call" | custom-call | tf_op jit(solution)/shard_map/prototypes/pallas_call | solution.py:327
Async XLA Ops:
  24.2 10.7 %all-to-all-start.1 = ((f32[8,96,128]{2,1,0:T(8,128)}), f32[8,96,128]{2,1,0:T(8,128)S(1)}, u32[]{:S(2)}, u32[]{:S(2)}) async-start(f32[8,96,128]{2,1,0:T(8,128)} %get-tuple-element.15), calls=%async_computation.1 | async-start | bytes 786432 | tf_op jit(solution)/shard_map/all_to_all | solution.py:266
  28.5 2.3 %copy-start = (bf16[3072,768]{1,0:T(8,128)(2,1)S(1)}, bf16[3072,768]{1,0:T(8,128)(2,1)}, u32[]{:S(2)}) copy-start(bf16[3072,768]{1,0:T(8,128)(2,1)} %rows_hbm.3) | copy-start | bytes 14155780
  39.1 11.7 %all-to-all-start.2 = ((f32[8,96,128]{2,1,0:T(8,128)}), f32[8,96,128]{2,1,0:T(8,128)S(1)}, u32[]{:S(2)}, u32[]{:S(2)}) async-start(f32[8,96,128]{2,1,0:T(8,128)} %get-tuple-element.20), calls=%async_computation.2 | async-start | bytes 786432 | tf_op jit(solution)/shard_map/all_to_all | solution.py:266
  44.3 1.8 %collective-permute-start.2 = (f32[3072]{0:T(1024)S(1)}, f32[3072]{0:T(1024)S(1)}, u32[]{:S(2)}, u32[]{:S(2)}) collective-permute-start(f32[3072]{0:T(1024)S(1)} %bitcast.2), channel_id=1, source_target_pairs={{0,3},{1,0},{2,1},{3,2},{4,7},{5,4},{6,5},{7,6},{8,11},{9,8},{10,9... | collective-permute-start | bytes 36872 | tf_op jit(solution)/shard_map/ppermute | solution.py:326
  44.3 3.7 %collective-permute-start.1 = (f32[3072]{0:T(1024)S(1)}, f32[3072]{0:T(1024)S(1)}, u32[]{:S(2)}, u32[]{:S(2)}) collective-permute-start(f32[3072]{0:T(1024)S(1)} %bitcast.3), channel_id=1, source_target_pairs={{0,2},{1,3},{2,0},{3,1},{4,6},{5,7},{6,4},{7,5},{8,10},{9,11},{10,... | collective-permute-start | bytes 36872 | tf_op jit(solution)/shard_map/ppermute | solution.py:326
  45.9 3.1 %collective-permute-start = (f32[3072]{0:T(1024)S(1)}, f32[3072]{0:T(1024)S(1)}, u32[]{:S(2)}, u32[]{:S(2)}) collective-permute-start(f32[3072]{0:T(1024)S(1)} %bitcast.4), channel_id=1, source_target_pairs={{0,1},{1,2},{2,3},{3,0},{4,5},{5,6},{6,7},{7,4},{8,9},{9,10},{10,1... | collective-permute-start | bytes 36872 | tf_op jit(solution)/shard_map/ppermute | solution.py:326

commit v7 on v6

--- a/solution.py
+++ b/solution.py
@@ -17,6 +17,8 @@
 
 VMEM = pl.BlockSpec(memory_space=pltpu.VMEM)
 HBM = pl.BlockSpec(memory_space=pltpu.MemorySpace.HBM)
+SHIP_PIECES = 2
+EIGHTHS = (4, 6, 0, 5, 2, 3, 1, 7)
 VMEM_LIMIT = 24 * 1024 * 1024
 
 
@@ -50,6 +52,25 @@
             ref[owner, piece * SLOTS:(piece + 1) * SLOTS, :] = rows[
                 owner * SLOTS:(owner + 1) * SLOTS, piece * LANES:(piece + 1) * LANES
             ]
+
+
+def ship_slots(out_hbm, out_ref, out_sems, make_rows):
+    owner_count, slot_rows = out_ref.shape[:2]
+    step = min(SHIP_PIECES, slot_rows // SLOTS)
+    copies = []
+    for t in range(slot_rows // SLOTS // step):
+        rows = make_rows(slice(t * step * LANES, (t + 1) * step * LANES))
+        for owner in range(owner_count):
+            for piece in range(step):
+                first = (t * step + piece) * SLOTS
+                out_ref[owner, first:first + SLOTS, :] = rows[
+                    owner * SLOTS:(owner + 1) * SLOTS, piece * LANES:(piece + 1) * LANES
+                ]
+        part = pl.ds(t * step * SLOTS, step * SLOTS)
+        copies.append(pltpu.make_async_copy(out_ref.at[:, part], out_hbm.at[:, part], out_sems.at[t]))
+        copies[-1].start()
+    for copy in copies:
+        copy.wait()
 
 
 def get_slots(ref, pieces):
@@ -182,9 +203,9 @@
         measure_rows(rows_ref, out_ref)
 
 
-def weigh_kernel(unit_ref, head_ref, rows_hbm, slot_ref, length_ref, out_ref, sim_ref, weight_ref, tail_ref, tail_sem):
+def weigh_kernel(unit_ref, head_ref, rows_hbm, slot_ref, length_ref, out_hbm, sim_ref, weight_ref, tail_ref, tail_sem, out_ref, out_sems):
     head_total, width = head_ref.shape
-    slot_total = out_ref.shape[0] * SLOTS
+    slot_total = out_hbm.shape[0] * SLOTS
     tail_copy = pltpu.make_async_copy(rows_hbm.at[pl.ds(head_total, tail_ref.shape[0])], tail_ref, tail_sem)
     tail_copy.start()
     units = jnp.concatenate(split2(get_slots(unit_ref, width // LANES)), axis=0)
@@ -204,9 +225,14 @@
     front, back = slice(0, head_total), slice(head_total, head_total + tail_ref.shape[0])
     weights_of(head_ref, front)
     tail_copy.wait()
-    total = dot(weight_ref[:, front], head_ref[...], ((1,), (0,)))
     weights_of(tail_ref, back)
-    put_slots(out_ref, total + dot(weight_ref[:, back], tail_ref[...], ((1,), (0,))))
+
+    def weighted(lanes):
+        return dot(weight_ref[:, front], head_ref[:, lanes], ((1,), (0,))) + dot(
+            weight_ref[:, back], tail_ref[:, lanes], ((1,), (0,))
+        )
+
+    ship_slots(out_hbm, out_ref, out_sems, weighted)
 
 
 def prototypes_kernel(got_ref, ids_ref, out_ref):
@@ -217,11 +243,11 @@
     out_ref[...] = unit[:out_ref.shape[0]]
 
 
-def call(kernel, ins, outs, name, scratch=(), cost=None):
+def call(kernel, ins, outs, name, scratch=(), cost=None, out_specs=None):
     return pl.pallas_call(
         kernel,
         in_specs=ins,
-        out_specs=[VMEM] * len(outs),
+        out_specs=out_specs or [VMEM] * len(outs),
         out_shape=[
             shape if isinstance(shape, jax.ShapeDtypeStruct) else jax.ShapeDtypeStruct(shape, jnp.float32)
             for shape in outs
@@ -238,10 +264,10 @@
 
 
 def owner_order(owner_count):
-    quarter = owner_count // 4
-    if owner_count % 4:
+    if owner_count % len(EIGHTHS):
         return list(range(owner_count))
-    return [*range(2 * quarter, 3 * quarter), *range(2 * quarter), *range(3 * quarter, owner_count)]
+    run = owner_count // len(EIGHTHS)
+    return [part * run + step for part in EIGHTHS for step in range(run)]
 
 
 def owner_at(place, owner_count):
@@ -316,7 +342,10 @@
             pltpu.VMEM((slot_total, row_total), jnp.bfloat16),
             pltpu.VMEM((row_total - head, width), jnp.bfloat16),
             pltpu.SemaphoreType.DMA,
+            pltpu.VMEM((owner_count, slot_rows, LANES), jnp.float32),
+            pltpu.SemaphoreType.DMA((pieces,)),
         ],
+        out_specs=[HBM, VMEM],
     )(units, head_rows, in_hbm(embeddings), where_to, lengths)
     got_weighted = exchange(weighted)
     own = own_similarity.reshape(row_total)

time: 52.2 us -> 51.5 us (0.987)
  waiting for transfers between devices: 7.94 us -> 6.92 us
  starting transfers between devices: 11.3 us -> 12.3 us
    all_to_all x2, waiting for transfers between devices: 5.04 us -> 4.03 us  [exchange(): lax.all_to_all(payload, 'dp', split_axis=0, concat_axis=0, tiled=True, ax...]
    all_to_all x2, starting transfers between devices: 9.59 us -> 10.6 us  [exchange(): lax.all_to_all(payload, 'dp', split_axis=0, concat_axis=0, tiled=True, ax...]
where the time goes in v7:
time: 51.5 us; the launch traced here: 51 us
  blocking collectives  15.2 us (30%)
  Pallas kernels  12.3 us (24%)
  starting transfers between devices  12.3 us (24%)
  waiting for transfers between devices  6.92 us (13%)
  local copies, waits for them, and re-layouts  2.34 us (5%)
  between operations  1.31 us (3%)
  other arithmetic  0.6 us (1%)
    all_to_all x1, blocking collectives, exchange(): lax.all_to_all(payload, 'dp', split_axis=0, concat_axis=0, tiled=True, ax...  15.2 us
    all_to_all x2, starting transfers between devices, exchange(): lax.all_to_all(payload, 'dp', split_axis=0, concat_axis=0, tiled=True, ax...  10.6 us
    pallas_call x1, Pallas kernels, shards(): call(functools.partial(sums_kernel, group_count), [pl.BlockSpec(memory_sp...  5.92 us
    all_to_all x2, waiting for transfers between devices, exchange(): lax.all_to_all(payload, 'dp', split_axis=0, concat_axis=0, tiled=True, ax...  4.03 us
    pallas_call x1, Pallas kernels, shards(): call(weigh_kernel, [VMEM, VMEM, HBM, VMEM, VMEM], [(owner_count, slot_row...  3.9 us
    ppermute x3, waiting for transfers between devices, shards(): similarity = similarity + lax.ppermute(own, 'cls', ring)  2.89 us
    unnamed x2, local copies, waits for them, and re-layouts  2.34 us
    ppermute x3, starting transfers between devices, shards(): similarity = similarity + lax.ppermute(own, 'cls', ring)  1.75 us
  transfers between devices with their start and end apart: 5, of which 4 were waited for; matrix products, arithmetic and copies ran while one was open for 1% of the time, Pallas kernels for 0%

profile of v7, /device:TPU:0, one launch (start us, length us, event | category | flops | bytes accessed | tf_op | source)
XLA Modules:
  0.0 51.0 jit_solution(5440707767095069146)
XLA Ops:
  1.3 5.9 %sums.1 = (f32[8,104,128]{2,1,0:T(8,128)S(1)}, f32[1,3072]{1,0:T(1,128)S(1)}, f32[1,3072]{1,0:T(1,128)S(1)}) custom-call(s32[1]{0:T(128)S(6)} %copy.6.live_ref, s32[1,3072]{1,0:T(1,128)} %bitcast.6, bf16[3072,768]{1,0:T(8,128)(2,1)} %rows_hbm.3), custom_call_target="tpu_custom_call" | custom-call | tf_op jit(solution)/shard_map/sums/pallas_call | solution.py:303
  7.2 15.2 %all_to_all.15.got_ref = f32[8,104,128]{2,1,0:T(8,128)S(1)} all-to-all(f32[8,104,128]{2,1,0:T(8,128)S(1)} %get-tuple-element.13), channel_id=1, replica_groups={{16,24,0,20,8,12,4,28},{17,25,1,21,9,13,5,29},{18,26,2,22,10,14,6,30},{..., dimensions={0} | all-to-all | bytes 851968 | tf_op jit(solution)/shard_map/all_to_all | solution.py:292
  22.4 1.3 %means.1 = (f32[86,768]{1,0:T(8,128)}, f32[8,96,128]{2,1,0:T(8,128)}, f32[1,128]{1,0:T(1,128)S(1)}) custom-call(f32[8,104,128]{2,1,0:T(8,128)S(1)} %all_to_all.15.got_ref), custom_call_target="tpu_custom_call" | custom-call | tf_op jit(solution)/shard_map/means/pallas_call | solution.py:329
  23.7 4.9 %all-to-all-start.1 = ((f32[8,96,128]{2,1,0:T(8,128)}), f32[8,96,128]{2,1,0:T(8,128)S(1)}, u32[]{:S(2)}, u32[]{:S(2)}) async-start(f32[8,96,128]{2,1,0:T(8,128)} %get-tuple-element.15), calls=%async_computation.1 | async-start | bytes 786432 | tf_op jit(solution)/shard_map/all_to_all | solution.py:292
  28.6 0.0 copy-start
  28.6 2.3 %copy-done = bf16[3072,768]{1,0:T(8,128)(2,1)S(1)} copy-done((bf16[3072,768]{1,0:T(8,128)(2,1)S(1)}, bf16[3072,768]{1,0:T(8,128)(2,1)}, u32[]{:S(2)}) %copy-start) | copy-done | bytes 4718616
  30.9 0.2 lengths.1
  31.1 3.4 %all-to-all-done.1.unit_ref = f32[8,96,128]{2,1,0:T(8,128)S(1)} async-done(((f32[8,96,128]{2,1,0:T(8,128)}), f32[8,96,128]{2,1,0:T(8,128)S(1)}, u32[]{:S(2)}, u32[]{:S(2)}) %all-to-all-start.1) | async-done | bytes 393248 | tf_op jit(solution)/shard_map/all_to_all | solution.py:292
  34.5 3.9 %weigh.1 = (f32[8,96,128]{2,1,0:T(8,128)}, f32[1,3072]{1,0:T(1,128)S(1)}) custom-call(f32[8,96,128]{2,1,0:T(8,128)S(1)} %all-to-all-done.1.unit_ref, bf16[1792,768]{1,0:T(8,128)(2,1)S(1)} %get-tuple-element.17.head_ref, bf16[3072,768]{1,0:T(8,128)(2,1)} %rows_hbm.3, f32[1,3072]{1,0:T(1,128)S(1)} %get-tuple-element.18.slot_ref, ...), custom_call_target="tpu_custom_call" | custom-call | tf_op jit(solution)/shard_map/weigh/pallas_call | solution.py:336
  38.4 5.7 %all-to-all-start.2 = ((f32[8,96,128]{2,1,0:T(8,128)}), f32[8,96,128]{2,1,0:T(8,128)S(1)}, u32[]{:S(2)}, u32[]{:S(2)}) async-start(f32[8,96,128]{2,1,0:T(8,128)} %get-tuple-element.20), calls=%async_computation.2 | async-start | bytes 786432 | tf_op jit(solution)/shard_map/all_to_all | solution.py:292
  44.1 0.0 collective-permute-start.2
  44.1 1.5 %collective-permute-start.1 = (f32[3072]{0:T(1024)S(1)}, f32[3072]{0:T(1024)S(1)}, u32[]{:S(2)}, u32[]{:S(2)}) collective-permute-start(f32[3072]{0:T(1024)S(1)} %bitcast.3), channel_id=1, source_target_pairs={{0,2},{1,3},{2,0},{3,1},{4,6},{5,7},{6,4},{7,5},{8,10},{9,11},{10,... | collective-permute-start | bytes 36872 | tf_op jit(solution)/shard_map/ppermute | solution.py:355
  45.6 0.2 collective-permute-start
  45.9 0.0 collective-permute-done.2
  45.9 1.9 %collective-permute-done.1 = f32[3072]{0:T(1024)S(1)} collective-permute-done((f32[3072]{0:T(1024)S(1)}, f32[3072]{0:T(1024)S(1)}, u32[]{:S(2)}, u32[]{:S(2)}) %collective-permute-start.1) | collective-permute-done | bytes 12320 | tf_op jit(solution)/shard_map/ppermute | solution.py:355
  47.8 0.9 %collective-permute-done = f32[3072]{0:T(1024)S(1)} collective-permute-done((f32[3072]{0:T(1024)S(1)}, f32[3072]{0:T(1024)S(1)}, u32[]{:S(2)}, u32[]{:S(2)}) %collective-permute-start) | collective-permute-done | bytes 12320 | tf_op jit(solution)/shard_map/ppermute | solution.py:355
  48.8 0.6 %add_add_fusion = f32[3072]{0:T(1024)} fusion(f32[3072]{0:T(1024)S(1)} %collective-permute-done.2, f32[3072]{0:T(1024)S(1)} %collective-permute-done.1, f32[3072]{0:T(1024)S(1)} %bitcast.5, f32[3072]{0:T(1024)S(1)} %collective-permute-done), kind=kLoop, calls=%fused_computation | loop fusion | flops 9216 | bytes 61440 | tf_op jit(solution)/shard_map/add | solution.py:355
  49.4 0.7 %all-to-all-done.2.got_ref = f32[8,96,128]{2,1,0:T(8,128)S(1)} async-done(((f32[8,96,128]{2,1,0:T(8,128)}), f32[8,96,128]{2,1,0:T(8,128)S(1)}, u32[]{:S(2)}, u32[]{:S(2)}) %all-to-all-start.2) | async-done | bytes 393248 | tf_op jit(solution)/shard_map/all_to_all | solution.py:292
  50.0 1.0 %prototypes.1 = f32[86,768]{1,0:T(8,128)} custom-call(f32[8,96,128]{2,1,0:T(8,128)S(1)} %all-to-all-done.2.got_ref, f32[1,128]{1,0:T(1,128)S(1)} %get-tuple-element.21.ids_ref), custom_call_target="tpu_custom_call" | custom-call | tf_op jit(solution)/shard_map/prototypes/pallas_call | solution.py:356
Async XLA Ops:
  23.7 10.8 %all-to-all-start.1 = ((f32[8,96,128]{2,1,0:T(8,128)}), f32[8,96,128]{2,1,0:T(8,128)S(1)}, u32[]{:S(2)}, u32[]{:S(2)}) async-start(f32[8,96,128]{2,1,0:T(8,128)} %get-tuple-element.15), calls=%async_computation.1 | async-start | bytes 786432 | tf_op jit(solution)/shard_map/all_to_all | solution.py:292
  28.6 2.3 %copy-start = (bf16[3072,768]{1,0:T(8,128)(2,1)S(1)}, bf16[3072,768]{1,0:T(8,128)(2,1)}, u32[]{:S(2)}) copy-start(bf16[3072,768]{1,0:T(8,128)(2,1)} %rows_hbm.3) | copy-start | bytes 14155780
  38.4 11.6 %all-to-all-start.2 = ((f32[8,96,128]{2,1,0:T(8,128)}), f32[8,96,128]{2,1,0:T(8,128)S(1)}, u32[]{:S(2)}, u32[]{:S(2)}) async-start(f32[8,96,128]{2,1,0:T(8,128)} %get-tuple-element.20), calls=%async_computation.2 | async-start | bytes 786432 | tf_op jit(solution)/shard_map/all_to_all | solution.py:292
  44.1 1.8 %collective-permute-start.2 = (f32[3072]{0:T(1024)S(1)}, f32[3072]{0:T(1024)S(1)}, u32[]{:S(2)}, u32[]{:S(2)}) collective-permute-start(f32[3072]{0:T(1024)S(1)} %bitcast.2), channel_id=1, source_target_pairs={{0,3},{1,0},{2,1},{3,2},{4,7},{5,4},{6,5},{7,6},{8,11},{9,8},{10,9... | collective-permute-start | bytes 36872 | tf_op jit(solution)/shard_map/ppermute | solution.py:355
  44.1 3.7 %collective-permute-start.1 = (f32[3072]{0:T(1024)S(1)}, f32[3072]{0:T(1024)S(1)}, u32[]{:S(2)}, u32[]{:S(2)}) collective-permute-start(f32[3072]{0:T(1024)S(1)} %bitcast.3), channel_id=1, source_target_pairs={{0,2},{1,3},{2,0},{3,1},{4,6},{5,7},{6,4},{7,5},{8,10},{9,11},{10,... | collective-permute-start | bytes 36872 | tf_op jit(solution)/shard_map/ppermute | solution.py:355
  45.6 3.1 %collective-permute-start = (f32[3072]{0:T(1024)S(1)}, f32[3072]{0:T(1024)S(1)}, u32[]{:S(2)}, u32[]{:S(2)}) collective-permute-start(f32[3072]{0:T(1024)S(1)} %bitcast.4), channel_id=1, source_target_pairs={{0,1},{1,2},{2,3},{3,0},{4,5},{5,6},{6,7},{7,4},{8,9},{9,10},{10,1... | collective-permute-start | bytes 36872 | tf_op jit(solution)/shard_map/ppermute | solution.py:355

commit v8 on v7

--- a/solution.py
+++ b/solution.py
@@ -154,10 +154,9 @@
         length_ref[...] = jnp.zeros_like(length_ref)
 
 
-def means_kernel(got_ref, means_ref, back_ref, ids_ref):
+def mean_rows(got_ref, width):
     owner_count = got_ref.shape[0]
     slot_total = owner_count * SLOTS
-    width = means_ref.shape[1]
     pieces = width // LANES
     metas = []
     for t in range(slot_total // LANES):
@@ -168,13 +167,16 @@
         metas.append(meta)
     meta = jnp.concatenate(metas, axis=1)
     ids = meta[0:1, :]
-    ids_ref[...] = ids
     match = iota((CLS_PAD, slot_total), 0) == ids
     counts = jnp.sum(jnp.where(match, meta[1:2, :], 0.0), axis=1, keepdims=True)
     onehot = flags(match)
     sums = pick(onehot, get_slots(got_ref, pieces), 1)
-    means = sums * (1.0 / jnp.maximum(counts, 1.0))
-    means_ref[...] = means[:means_ref.shape[0]]
+    return ids, onehot, sums * (1.0 / jnp.maximum(counts, 1.0))
+
+
+def units_kernel(got_ref, back_ref, ids_ref):
+    ids, onehot, means = mean_rows(got_ref, back_ref.shape[1] // SLOTS * LANES)
+    ids_ref[...] = ids
     unit = means * (1.0 / jnp.sqrt(jnp.sum(means * means, axis=1, keepdims=True) + epsilon))
     put_slots(back_ref, pick(onehot, unit, 0))
 
@@ -190,7 +192,8 @@
         out_ref[:, t * tile:(t + 1) * tile] = jnp.sqrt(total[0:1] + epsilon)
 
 
-def lengths_kernel(rows_ref, early_ref, out_ref, head_ref):
+def lengths_kernel(rows_ref, early_ref, got_ref, out_ref, head_ref, means_ref):
+    means_ref[...] = mean_rows(got_ref, means_ref.shape[1])[2][:means_ref.shape[0]]
     my_group = lax.axis_index("cls")
     head_ref[...] = rows_ref[:head_ref.shape[0], :]
 
@@ -318,19 +321,19 @@
     )(row_count, in_hbm(labels.reshape(1, row_total)), in_hbm(embeddings))
     got = exchange(payload)
     cost = pl.CostEstimate(flops=8 * row_total * width * 128, bytes_accessed=2 * row_total * width, transcendentals=row_total)
-    head = row_total * 7 // 12 // 256 * 256
-    lengths, head_rows = call(
+    head = row_total // 2
+    lengths, head_rows, class_means = call(
         lengths_kernel,
-        [VMEM, VMEM],
-        [(1, row_total), jax.ShapeDtypeStruct((head, width), jnp.bfloat16)],
+        [VMEM, VMEM, VMEM],
+        [(1, row_total), jax.ShapeDtypeStruct((head, width), jnp.bfloat16), (CLS_DEV, width)],
         "lengths",
         cost=cost,
-    )(embeddings, early_lengths)
-    class_means, back, ids = call(
-        means_kernel,
+    )(embeddings, early_lengths, got)
+    back, ids = call(
+        units_kernel,
         [VMEM],
-        [(CLS_DEV, width), (owner_count, slot_rows, LANES), (1, slot_total)],
-        "means",
+        [(owner_count, slot_rows, LANES), (1, slot_total)],
+        "units",
     )(got)
     units = exchange(back)
     weighted, own_similarity = call(

time: 51.5 us -> 51.6 us (level)
  waiting for transfers between devices: 6.92 us -> 4.9 us
  starting transfers between devices: 12.3 us -> 13.6 us
  Pallas kernels: 12.3 us -> 13.2 us
    ppermute x3, waiting for transfers between devices: 2.89 us -> 1.4 us  [shards(): similarity = similarity + lax.ppermute(own, 'cls', ring)]
    ppermute x3, starting transfers between devices: 1.75 us -> 2.98 us  [shards(): similarity = similarity + lax.ppermute(own, 'cls', ring)]
    pallas_call x2, Pallas kernels: 1.46 us -> 2.25 us  [the longest x1 1.28 us: shards(): call(units_kernel, [VMEM], [(owner_count, slot_rows, LANES), (1, slot_tot...]
    all_to_all x2, waiting for transfers between devices: 4.03 us -> 3.5 us  [exchange(): lax.all_to_all(payload, 'dp', split_axis=0, concat_axis=0, tiled=True, ax...]
  transfers between devices with their start and end apart: 5 -> 5, of which waited for: 4 -> 5; matrix products, arithmetic and copies ran while one was open for 1% -> 1% of each run, Pallas kernels for 0% -> 2%
where the time goes in v8:
time: 51.6 us; the launch traced here: 51.1 us
  blocking collectives  15.2 us (29%)
  starting transfers between devices  13.6 us (26%)
  Pallas kernels  13.2 us (26%)
  waiting for transfers between devices  4.9 us (9%)
  local copies, waits for them, and re-layouts  2.34 us (5%)
  between operations  1.3 us (3%)
  other arithmetic  0.6 us (1%)
    all_to_all x1, blocking collectives, exchange(): lax.all_to_all(payload, 'dp', split_axis=0, concat_axis=0, tiled=True, ax...  15.2 us
    all_to_all x2, starting transfers between devices, exchange(): lax.all_to_all(payload, 'dp', split_axis=0, concat_axis=0, tiled=True, ax...  10.6 us
    pallas_call x1, Pallas kernels, shards(): call(functools.partial(sums_kernel, group_count), [pl.BlockSpec(memory_sp...  5.92 us
    pallas_call x1, Pallas kernels, shards(): call(weigh_kernel, [VMEM, VMEM, HBM, VMEM, VMEM], [(owner_count, slot_row...  4.02 us
    all_to_all x2, waiting for transfers between devices, exchange(): lax.all_to_all(payload, 'dp', split_axis=0, concat_axis=0, tiled=True, ax...  3.5 us
    ppermute x3, starting transfers between devices, shards(): similarity = similarity + lax.ppermute(own, 'cls', ring)  2.98 us
    unnamed x2, local copies, waits for them, and re-layouts  2.34 us
    ppermute x3, waiting for transfers between devices, shards(): similarity = similarity + lax.ppermute(own, 'cls', ring)  1.4 us
  transfers between devices with their start and end apart: 5, of which 5 were waited for; matrix products, arithmetic and copies ran while one was open for 1% of the time, Pallas kernels for 2%

profile of v8, /device:TPU:0, one launch (start us, length us, event | category | flops | bytes accessed | tf_op | source)
XLA Modules:
  0.0 51.1 jit_solution(11130867743325704625)
XLA Ops:
  1.3 5.9 %sums.1 = (f32[8,104,128]{2,1,0:T(8,128)S(1)}, f32[1,3072]{1,0:T(1,128)S(1)}, f32[1,3072]{1,0:T(1,128)S(1)}) custom-call(s32[1]{0:T(128)S(6)} %copy.6.live_ref, s32[1,3072]{1,0:T(1,128)} %bitcast.6, bf16[3072,768]{1,0:T(8,128)(2,1)} %rows_hbm.3), custom_call_target="tpu_custom_call" | custom-call | tf_op jit(solution)/shard_map/sums/pallas_call | solution.py:306
  7.2 15.2 %all_to_all.15.got_ref = f32[8,104,128]{2,1,0:T(8,128)S(1)} all-to-all(f32[8,104,128]{2,1,0:T(8,128)S(1)} %get-tuple-element.14), channel_id=1, replica_groups={{16,24,0,20,8,12,4,28},{17,25,1,21,9,13,5,29},{18,26,2,22,10,14,6,30},{..., dimensions={0} | all-to-all | bytes 851968 | tf_op jit(solution)/shard_map/all_to_all | solution.py:295
  22.4 1.3 %units.1 = (f32[8,96,128]{2,1,0:T(8,128)}, f32[1,128]{1,0:T(1,128)S(1)}) custom-call(f32[8,104,128]{2,1,0:T(8,128)S(1)} %all_to_all.15.got_ref), custom_call_target="tpu_custom_call" | custom-call | tf_op jit(solution)/shard_map/units/pallas_call | solution.py:332
  23.7 4.9 %all-to-all-start.1 = ((f32[8,96,128]{2,1,0:T(8,128)}), f32[8,96,128]{2,1,0:T(8,128)S(1)}, u32[]{:S(2)}, u32[]{:S(2)}) async-start(f32[8,96,128]{2,1,0:T(8,128)} %get-tuple-element.16), calls=%async_computation.1 | async-start | bytes 786432 | tf_op jit(solution)/shard_map/all_to_all | solution.py:295
  28.6 0.0 copy-start
  28.6 2.3 %copy-done = bf16[3072,768]{1,0:T(8,128)(2,1)S(1)} copy-done((bf16[3072,768]{1,0:T(8,128)(2,1)S(1)}, bf16[3072,768]{1,0:T(8,128)(2,1)}, u32[]{:S(2)}) %copy-start) | copy-done | bytes 4718616
  30.9 1.0 %lengths.1 = (f32[1,3072]{1,0:T(1,128)S(1)}, bf16[1536,768]{1,0:T(8,128)(2,1)S(1)}, f32[86,768]{1,0:T(8,128)}) custom-call(bf16[3072,768]{1,0:T(8,128)(2,1)S(1)} %copy-done, f32[1,3072]{1,0:T(1,128)S(1)} %get-tuple-element.13.early_ref, f32[8,104,128]{2,1,0:T(8,128)S(1)} %all_to_all.15.got_ref), custom_call_target="tpu_custom_call" | custom-call | flops 2415919104 | bytes 4718592 | tf_op jit(solution)/shard_map/lengths/pallas_call | solution.py:325
  31.9 2.6 %all-to-all-done.1.unit_ref = f32[8,96,128]{2,1,0:T(8,128)S(1)} async-done(((f32[8,96,128]{2,1,0:T(8,128)}), f32[8,96,128]{2,1,0:T(8,128)S(1)}, u32[]{:S(2)}, u32[]{:S(2)}) %all-to-all-start.1) | async-done | bytes 393248 | tf_op jit(solution)/shard_map/all_to_all | solution.py:295
  34.5 4.0 %weigh.1 = (f32[8,96,128]{2,1,0:T(8,128)}, f32[1,3072]{1,0:T(1,128)S(1)}) custom-call(f32[8,96,128]{2,1,0:T(8,128)S(1)} %all-to-all-done.1.unit_ref, bf16[1536,768]{1,0:T(8,128)(2,1)S(1)} %get-tuple-element.17.head_ref, bf16[3072,768]{1,0:T(8,128)(2,1)} %rows_hbm.3, f32[1,3072]{1,0:T(1,128)S(1)} %get-tuple-element.18.slot_ref, ...), custom_call_target="tpu_custom_call" | custom-call | tf_op jit(solution)/shard_map/weigh/pallas_call | solution.py:339
  38.5 5.7 %all-to-all-start.2 = ((f32[8,96,128]{2,1,0:T(8,128)}), f32[8,96,128]{2,1,0:T(8,128)S(1)}, u32[]{:S(2)}, u32[]{:S(2)}) async-start(f32[8,96,128]{2,1,0:T(8,128)} %get-tuple-element.20), calls=%async_computation.2 | async-start | bytes 786432 | tf_op jit(solution)/shard_map/all_to_all | solution.py:295
  44.2 0.0 collective-permute-start
  44.2 1.5 %collective-permute-start.1 = (f32[3072]{0:T(1024)S(1)}, f32[3072]{0:T(1024)S(1)}, u32[]{:S(2)}, u32[]{:S(2)}) collective-permute-start(f32[3072]{0:T(1024)S(1)} %bitcast.3), channel_id=1, source_target_pairs={{0,2},{1,3},{2,0},{3,1},{4,6},{5,7},{6,4},{7,5},{8,10},{9,11},{10,... | collective-permute-start | bytes 36872 | tf_op jit(solution)/shard_map/ppermute | solution.py:358
  45.8 1.5 %collective-permute-start.2 = (f32[3072]{0:T(1024)S(1)}, f32[3072]{0:T(1024)S(1)}, u32[]{:S(2)}, u32[]{:S(2)}) collective-permute-start(f32[3072]{0:T(1024)S(1)} %bitcast.4), channel_id=1, source_target_pairs={{0,3},{1,0},{2,1},{3,2},{4,7},{5,4},{6,5},{7,6},{8,11},{9,8},{10,9... | collective-permute-start | bytes 36872 | tf_op jit(solution)/shard_map/ppermute | solution.py:358
  47.2 0.1 collective-permute-done
  47.3 0.6 %collective-permute-done.1 = f32[3072]{0:T(1024)S(1)} collective-permute-done((f32[3072]{0:T(1024)S(1)}, f32[3072]{0:T(1024)S(1)}, u32[]{:S(2)}, u32[]{:S(2)}) %collective-permute-start.1) | collective-permute-done | bytes 12320 | tf_op jit(solution)/shard_map/ppermute | solution.py:358
  47.9 0.7 %collective-permute-done.2 = f32[3072]{0:T(1024)S(1)} collective-permute-done((f32[3072]{0:T(1024)S(1)}, f32[3072]{0:T(1024)S(1)}, u32[]{:S(2)}, u32[]{:S(2)}) %collective-permute-start.2) | collective-permute-done | bytes 12320 | tf_op jit(solution)/shard_map/ppermute | solution.py:358
  48.6 0.6 %add_add_fusion = f32[3072]{0:T(1024)} fusion(f32[3072]{0:T(1024)S(1)} %collective-permute-done.2, f32[3072]{0:T(1024)S(1)} %collective-permute-done.1, f32[3072]{0:T(1024)S(1)} %bitcast.5, f32[3072]{0:T(1024)S(1)} %collective-permute-done), kind=kLoop, calls=%fused_computation | loop fusion | flops 9216 | bytes 61440 | tf_op jit(solution)/shard_map/add | solution.py:358
  49.2 0.9 %all-to-all-done.2.got_ref = f32[8,96,128]{2,1,0:T(8,128)S(1)} async-done(((f32[8,96,128]{2,1,0:T(8,128)}), f32[8,96,128]{2,1,0:T(8,128)S(1)}, u32[]{:S(2)}, u32[]{:S(2)}) %all-to-all-start.2) | async-done | bytes 393248 | tf_op jit(solution)/shard_map/all_to_all | solution.py:295
  50.1 1.0 %prototypes.1 = f32[86,768]{1,0:T(8,128)} custom-call(f32[8,96,128]{2,1,0:T(8,128)S(1)} %all-to-all-done.2.got_ref, f32[1,128]{1,0:T(1,128)S(1)} %get-tuple-element.21.ids_ref), custom_call_target="tpu_custom_call" | custom-call | tf_op jit(solution)/shard_map/prototypes/pallas_call | solution.py:359
Async XLA Ops:
  23.7 10.8 %all-to-all-start.1 = ((f32[8,96,128]{2,1,0:T(8,128)}), f32[8,96,128]{2,1,0:T(8,128)S(1)}, u32[]{:S(2)}, u32[]{:S(2)}) async-start(f32[8,96,128]{2,1,0:T(8,128)} %get-tuple-element.16), calls=%async_computation.1 | async-start | bytes 786432 | tf_op jit(solution)/shard_map/all_to_all | solution.py:295
  28.6 2.3 %copy-start = (bf16[3072,768]{1,0:T(8,128)(2,1)S(1)}, bf16[3072,768]{1,0:T(8,128)(2,1)}, u32[]{:S(2)}) copy-start(bf16[3072,768]{1,0:T(8,128)(2,1)} %rows_hbm.3) | copy-start | bytes 14155780
  38.5 11.6 %all-to-all-start.2 = ((f32[8,96,128]{2,1,0:T(8,128)}), f32[8,96,128]{2,1,0:T(8,128)S(1)}, u32[]{:S(2)}, u32[]{:S(2)}) async-start(f32[8,96,128]{2,1,0:T(8,128)} %get-tuple-element.20), calls=%async_computation.2 | async-start | bytes 786432 | tf_op jit(solution)/shard_map/all_to_all | solution.py:295
  44.2 3.1 %collective-permute-start = (f32[3072]{0:T(1024)S(1)}, f32[3072]{0:T(1024)S(1)}, u32[]{:S(2)}, u32[]{:S(2)}) collective-permute-start(f32[3072]{0:T(1024)S(1)} %bitcast.2), channel_id=1, source_target_pairs={{0,1},{1,2},{2,3},{3,0},{4,5},{5,6},{6,7},{7,4},{8,9},{9,10},{10,1... | collective-permute-start | bytes 36872 | tf_op jit(solution)/shard_map/ppermute | solution.py:358
  44.2 3.7 %collective-permute-start.1 = (f32[3072]{0:T(1024)S(1)}, f32[3072]{0:T(1024)S(1)}, u32[]{:S(2)}, u32[]{:S(2)}) collective-permute-start(f32[3072]{0:T(1024)S(1)} %bitcast.3), channel_id=1, source_target_pairs={{0,2},{1,3},{2,0},{3,1},{4,6},{5,7},{6,4},{7,5},{8,10},{9,11},{10,... | collective-permute-start | bytes 36872 | tf_op jit(solution)/shard_map/ppermute | solution.py:358
  45.8 2.9 %collective-permute-start.2 = (f32[3072]{0:T(1024)S(1)}, f32[3072]{0:T(1024)S(1)}, u32[]{:S(2)}, u32[]{:S(2)}) collective-permute-start(f32[3072]{0:T(1024)S(1)} %bitcast.4), channel_id=1, source_target_pairs={{0,3},{1,0},{2,1},{3,2},{4,7},{5,4},{6,5},{7,6},{8,11},{9,8},{10,9... | collective-permute-start | bytes 36872 | tf_op jit(solution)/shard_map/ppermute | solution.py:358
